TPU v7x, 32 devices: a whole 2x2x4 slice. The times are simulated.
32 devices in a mesh: seq: 8 (over y, x, core), head: 4 (over z).
Axes of the slice: x: 2, y: 2, z: 4, core: 2. Of those that a mesh axis runs over, the one named last changes fastest.
Arguments:
- queries: bfloat16 [1024, 8192], P('seq', 'head'), may hold values from -2.5 to 2.5
- keys: bfloat16 [1024, 8192], P('seq', 'head'), may hold values from -2.5 to 2.5
- values: bfloat16 [1024, 4096], P('seq', 'head'), may hold values from -2.5 to 2.5
- out_grad: bfloat16 [1024, 4096], P('seq', 'head'), may hold values from -2.5 to 2.5
- log_gate: float32 [64, 1024], P('head', 'seq'), may hold values from -1 to 0
- level_weight: float32 [6, 64, 1024], P(None, 'head', 'seq'), may hold values from 0.25 to 2
- doc_start: int32 [1024], P('seq'), may hold values 0 or 1
Outputs:
- grad_queries: bfloat16 [1024, 8192], P('seq', 'head')
- grad_keys: bfloat16 [1024, 8192], P('seq', 'head')
- grad_values: bfloat16 [1024, 4096], P('seq', 'head')
- grad_level_weight: float32 [6, 64, 1024], P(None, 'head', 'seq')
- grad_log_gate: float32 [64, 1024], P('head', 'seq')
All inputs are finite; a program needn't handle non-finite values. No bound on the sum of `doc_start` on one device may be relied on, other than what follows from the above.
Results may differ from a plain program's by a relative error of at most 0.0027.
Values sent between devices are 32-bit elements; how exact they have to be, the bound alone decides.
A program may use at most 128 MiB of HBM per device.

v0:
```python
import functools

import jax
import jax.numpy as jnp
from jax import lax
from jax.experimental import pallas as pl
from jax.experimental.pallas import tpu as pltpu
from jax.sharding import PartitionSpec as P

SPAN = 64
F32 = jnp.float32
BF16 = jnp.bfloat16
NN = (((1,), (0,)), ((), ()))
NT = (((1,), (1,)), ((), ()))
TN = (((0,), (0,)), ((), ()))
MESH = pl.DeviceIdType.MESH


def dot(a, b, dims):
    return lax.dot_general(a, b, dims, preferred_element_type=F32)


def split(x):
    high = x.astype(BF16)
    return high, (x - high.astype(F32)).astype(BF16)


def dot_fine(x, b, dims):
    high, low = split(x)
    return dot(high, b, dims) + dot(low, b, dims)


def span_level(a, b, levels):
    return 0 if a == b else min(levels - 1, (a ^ b).bit_length())


def kernel(
    seq_count,
    head_count,
    q_ref,
    k_ref,
    v_ref,
    g_ref,
    lg_ref,
    lw_ref,
    ds_ref,
    gq_ref,
    gk_ref,
    gv_ref,
    gl_ref,
    gg_ref,
    cum_s,
    col_s,
    lead_s,
    tail_s,
    bias_s,
    vt_s,
    gt_s,
    vg_s,
    gq_s,
    gk_s,
    drift_s,
    coef_s,
    state_s,
    back_s,
    lvl,
    got_s,
    got_u,
    sum_s,
    sum_u,
    dec,
    got_dec,
    tot,
    sq,
    lvl_send,
    lvl_recv,
    fwd_send,
    fwd_recv,
    s_send,
    s_recv,
    u_send,
    u_recv,
    d_send,
    d_recv,
    t_send,
    t_recv,
    q_send,
    q_recv,
):
    tok = q_ref.shape[0]
    heads = lg_ref.shape[0]
    levels = lw_ref.shape[0]
    dk = q_ref.shape[1] // heads
    dv = v_ref.shape[1] // heads
    group = dk // dv
    pairs = heads // group
    spans = tok // SPAN
    span_bits = spans.bit_length() - 1
    bits = seq_count.bit_length() - 1
    half = heads // 2
    cross = [min(span_bits + 1 + b, levels - 1) for b in range(bits)]
    slots = sorted(set(cross))
    place = lax.axis_index("seq")
    row = lax.axis_index("head")
    bit = [(place // (1 << b)) % 2 for b in range(bits)]
    peer = [place + (1 - 2 * bit[b]) * (1 << b) for b in range(bits)]
    want_s = [(place // (2 << b)) != (seq_count // (2 << b)) - 1 for b in range(bits)]
    mine = bit[0] * half
    theirs = (1 - bit[0]) * half

    barrier = pltpu.get_barrier_semaphore()
    for o in range(1, seq_count):
        pl.semaphore_signal(
            barrier, inc=1, device_id={"seq": (place + o) % seq_count}, device_id_type=MESH
        )
    for o in range(1, head_count):
        pl.semaphore_signal(
            barrier, inc=1, device_id={"head": (row + o) % head_count}, device_id_type=MESH
        )

    rows_i = lax.broadcasted_iota(jnp.int32, (tok, tok), 0)
    cols_i = lax.broadcasted_iota(jnp.int32, (tok, tok), 1)
    tri = (rows_i <= cols_i).astype(F32)
    starts = jnp.broadcast_to(ds_ref[...].astype(F32), (8, tok))
    both = jnp.concatenate([lg_ref[...], starts], axis=0)
    cum_all = lax.dot_general(
        both, tri, NN, precision=lax.Precision.HIGHEST, preferred_element_type=F32
    )
    cum_t = jnp.transpose(cum_all)
    cum = cum_all[:heads]
    reset = cum_all[heads : heads + 1]
    reset_col = cum_t[:, heads : heads + 1]
    bias_s[...] = jnp.where((rows_i <= cols_i) & (reset == reset_col), 0.0, -1e30)
    end = cum[:, tok - 1 : tok]
    reset_end = reset[:, tok - 1 : tok]
    cum_s[...] = cum
    lead_s[...] = jnp.where(reset == 0, jnp.exp(cum), 0.0)
    tail_s[...] = jnp.where(reset == reset_end, jnp.exp(end - cum), 0.0)
    dec[0] = jnp.broadcast_to(jnp.where(reset_end == 0, jnp.exp(end), 0.0), (heads, dk))
    for h in range(heads):
        col_s[h] = jnp.broadcast_to(cum_t[:, h : h + 1], (tok, tok))

    def states(p, _):
        lanes = pl.ds(pl.multiple_of(p * dk, dk), dk)
        vt = jnp.transpose(v_ref[:, lanes].astype(F32))
        gt = jnp.transpose(g_ref[:, lanes].astype(F32))
        vt_s[p] = vt.astype(BF16)
        gt_s[p] = gt.astype(BF16)
        for i in range(group):
            h = p * group + i
            wide = pl.ds(pl.multiple_of(h * dk, dk), dk)
            part = slice(i * dv, (i + 1) * dv)
            tail = tail_s[pl.ds(h, 1), :]
            lead = lead_s[pl.ds(h, 1), :]
            state_s[h] = dot_fine(vt[part] * tail, k_ref[:, wide], NN)
            gw = jnp.concatenate(
                [gt[part] * (lead * lw_ref[l, pl.ds(h, 1), :]) for l in slots], axis=0
            )
            back = dot_fine(gw, q_ref[:, wide], NN)
            for n in range(len(slots)):
                back_s[n, h] = back[n * dv : (n + 1) * dv]
        return 0

    lax.fori_loop(0, pairs, states, 0, unroll=2)
    pl.semaphore_wait(barrier, seq_count - 1 + head_count - 1)

    def slot(b):
        return slots.index(cross[b])

    def remote(src, dst, send, recv, b):
        return pltpu.make_async_remote_copy(
            src_ref=src,
            dst_ref=dst,
            send_sem=send,
            recv_sem=recv,
            device_id={"seq": peer[b]},
            device_id_type=MESH,
        )

    own = pl.ds(mine, half)
    other = pl.ds(theirs, half)

    def u_copy(b, j):
        src = back_s.at[slot(j), other] if b == 0 else sum_u.at[b, j]
        return remote(src, got_u.at[b, j], u_send.at[b, j], u_recv.at[b, j], b)

    def s_copy(b):
        src = state_s.at[other] if b == 0 else sum_s.at[b]
        return remote(src, got_s.at[b], s_send.at[b], s_recv.at[b], b)

    def d_copy(b):
        return remote(dec.at[b], got_dec.at[b], d_send.at[b], d_recv.at[b], b)

    def level_copy(b, low):
        if b == 0:
            src = state_s if low else back_s.at[slot(0)]
            return [
                remote(src.at[part], lvl.at[0, part], lvl_send.at[0, n], lvl_recv.at[0, n], 0)
                for n, part in enumerate((other, own))
            ]
        src = sum_s.at[b] if low else sum_u.at[b, b]
        return [remote(src, lvl.at[b, own], lvl_send.at[b, 0], lvl_recv.at[b, 0], b)]

    def level_wait(b, n):
        part = other if n == 1 else own
        return remote(
            lvl.at[b, part], lvl.at[b, part], lvl_send.at[b, n], lvl_recv.at[b, n], b
        )

    def forward_copy(b, part):
        return remote(lvl.at[b, part], lvl.at[b, part], fwd_send.at[b], fwd_recv.at[b], 0)

    def land(b):
        up_summed = (bit[b] == 1) & want_s[b]

        @pl.when(jnp.logical_not(up_summed))
        def _():
            level_wait(b, 0).wait_recv()

        if b > 0:
            forward_copy(b, own).start()

    def begin(b):
        d_copy(b).start()

        early = 0 if b in (0, bits - 1) else 1

        @pl.when((bit[b] == 0) & (want_s[b] | (early == 0)))
        def _():
            for c in level_copy(b, True):
                c.start()

        if b < bits - 1:

            @pl.when((bit[b] == 1) & want_s[b])
            def _():
                s_copy(b).start()

            for j in range(b + 1, bits):

                @pl.when(bit[j] == 1)
                def _(j=j):
                    u_copy(b, j).start()

        if early == 0:

            @pl.when(bit[b] == 1)
            def _():
                for c in level_copy(b, False):
                    c.start()

    def begin_late(b):
        if b in (0, bits - 1):
            return

        @pl.when((bit[b] == 0) & jnp.logical_not(want_s[b]))
        def _():
            for c in level_copy(b, True):
                c.start()

        @pl.when(bit[b] == 1)
        def _():
            for c in level_copy(b, False):
                c.start()

    def join(b):
        d_copy(b).wait_recv()
        up = bit[b].astype(F32)
        got = got_dec[b]
        now = dec[b]
        dec[b + 1] = got * now
        if b == bits - 1:
            return
        base_s = state_s.at[own] if b == 0 else sum_s.at[b]

        @pl.when(want_s[b])
        def _():
            @pl.when(bit[b] == 1)
            def _():
                level_wait(b, 0).wait_recv()

                def body(i, _):
                    d = dec[b, pl.ds(mine + i, 1), :]
                    sum_s[b + 1, i] = d * lvl[b, mine + i] + base_s[i]
                    return 0

                lax.fori_loop(0, half, body, 0, unroll=True)

            @pl.when(bit[b] == 0)
            def _():
                s_copy(b).wait_recv()

                def body(i, _):
                    d = got_dec[b, pl.ds(mine + i, 1), :]
                    sum_s[b + 1, i] = d * base_s[i] + got_s[b, i]
                    return 0

                lax.fori_loop(0, half, body, 0, unroll=True)

        for j in range(b + 1, bits):
            base_u = back_s.at[slot(j), own] if b == 0 else sum_u.at[b, j]

            @pl.when(bit[j] == 1)
            def _(j=j, base_u=base_u):
                u_copy(b, j).wait_recv()

                def body(i, _):
                    d0 = dec[b, pl.ds(mine + i, 1), :]
                    d1 = got_dec[b, pl.ds(mine + i, 1), :]
                    a = up * d1 + (1.0 - up)
                    c = (1.0 - up) * d0 + up
                    sum_u[b + 1, j, i] = a * base_u[i] + c * got_u[b, j, i]
                    return 0

                lax.fori_loop(0, half, body, 0, unroll=True)

    span_of = lax.broadcasted_iota(jnp.int32, (1, tok), 1) // SPAN

    def local(p, _):
        vt = vt_s[p]
        gt = gt_s[p]
        lanes = pl.ds(pl.multiple_of(p * dk, dk), dk)
        v_blk = v_ref[:, lanes]
        for i in range(group):
            h = p * group + i
            wide = pl.ds(pl.multiple_of(h * dk, dk), dk)
            part = slice(i * dv, (i + 1) * dv)
            q = q_ref[:, wide]
            k = k_ref[:, wide]
            score = dot(k, q, NT)
            pair = dot(v_blk[:, part], gt[part], NN)
            decay = jnp.exp((cum_s[pl.ds(h, 1), :] - col_s[h]) + bias_s[...])
            seen = decay * score
            both_p = seen * pair
            gains = [lw_ref[l, pl.ds(h, 1), :] for l in range(span_bits + 1)]
            level_rows = [jnp.zeros((1, tok), F32) for _ in range(span_bits + 1)]
            mixed, graded = [], []
            for cs in range(spans):
                rows = slice(cs * SPAN, (cs + 1) * SPAN)
                total = jnp.sum(both_p[rows], axis=0, keepdims=True)
                gain = jnp.zeros((1, tok), F32)
                for ct in range(cs, spans):
                    l = span_level(cs, ct, levels)
                    hit = span_of == ct
                    gain = jnp.where(hit, gains[l], gain)
                    level_rows[l] = level_rows[l] + jnp.where(hit, total, 0.0)
                mixed.append(seen[rows] * gain)
                graded.append(decay[rows] * gain * pair[rows])
            mix = jnp.concatenate(mixed, axis=0).astype(BF16)
            grade = jnp.concatenate(graded, axis=0).astype(BF16)
            for l in range(span_bits + 1):
                gl_ref[l, pl.ds(h, 1), :] = level_rows[l]
            drift_s[pl.ds(h, 1), :] = jnp.sum(mix.astype(F32) * pair, axis=0, keepdims=True)
            vg_s[p, part] = dot(gt[part], mix, NT)
            gk_s[h] = dot(grade, q, NN)
            gq_s[h] = dot(grade, k, TN)
        return 0

    begin(0)
    lax.fori_loop(0, pairs // 4, local, 0, unroll=2)
    join(0)
    if bits > 1:
        begin(1)
    lax.fori_loop(pairs // 4, pairs, local, 0, unroll=2)
    for b in range(1, bits):
        join(b)
        if b + 1 < bits:
            begin(b + 1)
        begin_late(b)
        land(b - 1)
    land(bits - 1)

    inner_f = jnp.ones((heads, dk), F32)
    inner_b = jnp.ones((heads, dk), F32)
    for b in range(bits):
        up = bit[b].astype(F32)
        got = got_dec[b]
        coef_s[0, b] = inner_f * up
        coef_s[1, b] = inner_b * (1.0 - up)
        inner_f = inner_f * (up * got + (1.0 - up))
        inner_b = inner_b * ((1.0 - up) * got + up)
    level_wait(0, 1).wait_recv()
    for b in range(1, bits):
        forward_copy(b, other).wait_recv()

    def finish(p, _):
        lanes = pl.ds(pl.multiple_of(p * dk, dk), dk)
        vt = vt_s[p].astype(F32)
        gt = gt_s[p].astype(F32)
        vg_all = []
        for i in range(group):
            h = p * group + i
            wide = pl.ds(pl.multiple_of(h * dk, dk), dk)
            part = slice(i * dv, (i + 1) * dv)
            q = q_ref[:, wide]
            k = k_ref[:, wide]
            tail = tail_s[pl.ds(h, 1), :]
            lead = lead_s[pl.ds(h, 1), :]
            blocks = [lvl[b, h] for b in range(bits)]
            entering = []
            for n in range(len(slots)):
                terms = [
                    coef_s[0, b, pl.ds(h, 1), :] * blocks[b] for b in range(bits) if slot(b) == n
                ]
                entering.append(functools.reduce(jnp.add, terms))
            entering = jnp.concatenate(entering, axis=0)
            after = functools.reduce(
                jnp.add, [coef_s[1, b, pl.ds(h, 1), :] * blocks[b] for b in range(bits)]
            )
            e_high, e_low = split(entering)
            seen = dot(e_high, q, NT) + dot(e_low, q, NT)
            drift = drift_s[pl.ds(h, 1), :]
            gws = []
            for n, l in enumerate(slots):
                gain = lw_ref[l, pl.ds(h, 1), :]
                level = lead * jnp.sum(
                    seen[n * dv : (n + 1) * dv] * gt[part], axis=0, keepdims=True
                )
                gl_ref[l, pl.ds(h, 1), :] = level
                drift = drift + gain * level
                gws.append(gt[part] * (lead * gain))
            gw, gw_low = split(jnp.concatenate(gws, axis=0))
            gq_in = dot(gw, e_high, TN) + dot(gw, e_low, TN) + dot(gw_low, e_high, TN)
            gq_ref[:, wide] = (gq_s[h] + gq_in).astype(BF16)
            a_high, a_low = split(after)
            tv, tv_low = split(vt[part] * tail)
            gk_in = dot(tv, a_high, TN) + dot(tv, a_low, TN) + dot(tv_low, a_high, TN)
            gk_ref[:, wide] = (gk_s[h] + gk_in).astype(BF16)
            vg = vg_s[p, part] + tail * (dot(a_high, k, NT) + dot(a_low, k, NT))
            drift_s[pl.ds(h, 1), :] = drift - jnp.sum(vg * vt[part], axis=0, keepdims=True)
            vg_all.append(vg)
        gv_ref[:, lanes] = jnp.transpose(jnp.concatenate(vg_all, axis=0)).astype(BF16)
        return 0

    lax.fori_loop(0, pairs, finish, 0, unroll=2)
    for l in range(levels):
        if l > span_bits and l not in slots:
            gl_ref[l] = jnp.zeros((heads, tok), F32)

    later = (rows_i >= cols_i).astype(F32)
    local_tail = lax.dot_general(
        drift_s[...], later, NN, precision=lax.Precision.HIGHEST, preferred_element_type=F32
    )
    lane = lax.broadcasted_iota(jnp.int32, (heads, tok), 1)
    first = local_tail[:, 0:1]
    plain = jnp.sum(local_tail, axis=1, keepdims=True)
    square = jnp.sum(local_tail * local_tail, axis=1, keepdims=True)
    tot[place] = jnp.where(lane == 0, first, jnp.where(lane == 1, plain, square))

    def tot_copy(o, slot_at):
        return pltpu.make_async_remote_copy(
            src_ref=tot.at[place],
            dst_ref=tot.at[slot_at],
            send_sem=t_send.at[o],
            recv_sem=t_recv.at[slot_at],
            device_id={"seq": (place + o) % seq_count},
            device_id_type=MESH,
        )

    for o in range(1, seq_count):
        tot_copy(o, place).start()
    for o in range(1, seq_count):
        tot_copy(o, (place + o) % seq_count).wait_recv()
    after_total = jnp.zeros((heads, 1), F32)
    my_later = jnp.zeros((heads, 1), F32)
    energy = jnp.zeros((heads, 1), F32)
    for d in reversed(range(seq_count)):
        piece = tot[d]
        my_later = my_later + jnp.where(place == d, 1.0, 0.0) * after_total
        energy = energy + (
            piece[:, 2:3] + after_total * (2.0 * piece[:, 1:2] + tok * after_total)
        )
        after_total = after_total + piece[:, 0:1]
    energy = jnp.sum(jnp.broadcast_to(energy, (heads, dk)), axis=0, keepdims=True)
    sq[row] = jnp.broadcast_to(energy, (8, dk))

    def sq_copy(o, slot_at):
        return pltpu.make_async_remote_copy(
            src_ref=sq.at[row],
            dst_ref=sq.at[slot_at],
            send_sem=q_send.at[o],
            recv_sem=q_recv.at[slot_at],
            device_id={"head": (row + o) % head_count},
            device_id_type=MESH,
        )

    for o in range(1, head_count):
        sq_copy(o, row).start()
    for o in range(1, head_count):
        sq_copy(o, (row + o) % head_count).wait_recv()
    whole = sq[0]
    for r in range(1, head_count):
        whole = whole + sq[r]
    count = heads * tok * seq_count * head_count
    factor = jnp.minimum(1.0, lax.rsqrt(whole[0:1] / count + 1e-6))
    gg_ref[...] = (local_tail + my_later) * factor

    for b in range(bits):
        d_copy(b).wait_send()
        for n in range(2 if b == 0 else 1):
            level_wait(b, n).wait_send()
        if b > 0:
            forward_copy(b, own).wait_send()
        if b < bits - 1:

            @pl.when((bit[b] == 1) & want_s[b])
            def _(b=b):
                s_copy(b).wait_send()

            for j in range(b + 1, bits):

                @pl.when(bit[j] == 1)
                def _(b=b, j=j):
                    u_copy(b, j).wait_send()

    for o in range(1, seq_count):
        tot_copy(o, place).wait_send()
    for o in range(1, head_count):
        sq_copy(o, row).wait_send()


def shards(seq_count, head_count, queries, keys, values, out_grad, log_gate, level_weight, doc_start):
    tok = queries.shape[0]
    heads = log_gate.shape[0]
    levels = level_weight.shape[0]
    dk = queries.shape[1] // heads
    dv = values.shape[1] // heads
    group = dk // dv
    pairs = heads // group
    bits = seq_count.bit_length() - 1
    half = heads // 2
    span_bits = (tok // SPAN).bit_length() - 1
    slots = len({min(span_bits + 1 + b, levels - 1) for b in range(bits)})
    dma = pltpu.SemaphoreType.DMA
    vmem = pltpu.VMEM
    block = (dv, dk)
    scratch = [
        vmem((heads, tok), F32),
        vmem((heads, tok, tok), F32),
        vmem((heads, tok), F32),
        vmem((heads, tok), F32),
        vmem((tok, tok), F32),
        vmem((pairs, group * dv, tok), BF16),
        vmem((pairs, group * dv, tok), BF16),
        vmem((pairs, group * dv, tok), F32),
        vmem((heads, tok, dk), F32),
        vmem((heads, tok, dk), F32),
        vmem((heads, tok), F32),
        vmem((2, bits, heads, dk), F32),
        vmem((heads,) + block, F32),
        vmem((slots, heads) + block, F32),
        vmem((bits, heads) + block, F32),
        vmem((bits, half) + block, F32),
        vmem((bits, bits, half) + block, F32),
        vmem((bits, half) + block, F32),
        vmem((bits, bits, half) + block, F32),
        vmem((bits + 1, heads, dk), F32),
        vmem((bits, heads, dk), F32),
        vmem((seq_count, heads, tok), F32),
        vmem((head_count, 8, dk), F32),
        dma((bits, 2)),
        dma((bits, 2)),
        dma((bits,)),
        dma((bits,)),
        dma((bits,)),
        dma((bits,)),
        dma((bits, bits)),
        dma((bits, bits)),
        dma((bits,)),
        dma((bits,)),
        dma((seq_count,)),
        dma((seq_count,)),
        dma((head_count,)),
        dma((head_count,)),
    ]
    spec = pl.BlockSpec(memory_space=pltpu.VMEM)
    return pl.pallas_call(
        functools.partial(kernel, seq_count, head_count),
        out_shape=(
            jax.ShapeDtypeStruct(queries.shape, BF16),
            jax.ShapeDtypeStruct(keys.shape, BF16),
            jax.ShapeDtypeStruct(values.shape, BF16),
            jax.ShapeDtypeStruct(level_weight.shape, F32),
            jax.ShapeDtypeStruct(log_gate.shape, F32),
        ),
        in_specs=[spec] * 7,
        out_specs=(spec,) * 5,
        scratch_shapes=scratch,
        compiler_params=pltpu.CompilerParams(collective_id=0, has_side_effects=True),
    )(queries, keys, values, out_grad, log_gate, level_weight, doc_start.reshape(1, tok))


def solution(mesh):
    return jax.shard_map(
        functools.partial(shards, mesh.shape["seq"], mesh.shape["head"]),
        mesh=mesh,
        in_specs=(
            P("seq", "head"),
            P("seq", "head"),
            P("seq", "head"),
            P("seq", "head"),
            P("head", "seq"),
            P(None, "head", "seq"),
            P("seq"),
        ),
        out_specs=(
            P("seq", "head"),
            P("seq", "head"),
            P("seq", "head"),
            P(None, "head", "seq"),
            P("head", "seq"),
        ),
        check_vma=False,
    )
```

profile of v0, /device:TPU:0, one launch (start us, length us, event | category | flops | bytes accessed | tf_op | source)
XLA Modules:
  0.0 44.6 jit_solution(12261945428217930794)
XLA Ops:
  0.6 38.9 %shard_map.110 = (bf16[128,2048]{1,0:T(8,128)(2,1)}, bf16[128,2048]{1,0:T(8,128)(2,1)}, bf16[128,1024]{1,0:T(8,128)(2,1)}, f32[6,16,128]{2,1,0:T(8,128)}, f32[16,128]{1,0:T(8,128)}) custom-call(bf16[128,2048]{1,0:T(8,128)(2,1)} %q_ref.1, bf16[128,2048]{1,0:T(8,128)(2,1)} %k_ref.1, bf16[128,1024]{1,0:T(8,128)(2,1)} %v_ref.1, bf16[128,1024]{1,0:T(8,128)(2,1)} %g_ref.1, ...), custom_call_target="tpu_custom_call" | custom-call | tf_op jit(solution)/shard_map/pallas_call | solution.py:577
  39.5 0.0 copy-start
  39.5 1.9 %copy.17 = bf16[128,2048]{1,0:T(8,128)(2,1)} copy(bf16[128,2048]{1,0:T(8,128)(2,1)} %get-tuple-element.10) | data formatting | bytes 1048576
  41.4 0.0 copy-done
  41.5 0.0 copy-start.1
  41.5 0.8 %copy.18 = bf16[128,2048]{1,0:T(8,128)(2,1)} copy(bf16[128,2048]{1,0:T(8,128)(2,1)S(1)} %copy-done) | data formatting | bytes 1048576
  42.2 0.3 copy-done.1
  42.5 0.0 copy-start.2
  42.5 0.7 %copy.19 = bf16[128,1024]{1,0:T(8,128)(2,1)} copy(bf16[128,1024]{1,0:T(8,128)(2,1)S(1)} %copy-done.1) | data formatting | bytes 524288
  43.2 0.1 copy-done.2
  43.3 0.0 copy-start.3
  43.3 0.6 %copy.20 = f32[6,16,128]{2,1,0:T(8,128)} copy(f32[6,16,128]{2,1,0:T(8,128)S(1)} %copy-done.2) | data formatting | bytes 98304
  44.0 0.1 copy-done.3
  44.0 0.6 %copy.21 = f32[16,128]{1,0:T(8,128)} copy(f32[16,128]{1,0:T(8,128)S(1)} %copy-done.3) | data formatting | bytes 16384
Async XLA Ops:
  39.5 2.0 %copy-start = (bf16[128,2048]{1,0:T(8,128)(2,1)S(1)}, bf16[128,2048]{1,0:T(8,128)(2,1)}, u32[]{:S(2)}) copy-start(bf16[128,2048]{1,0:T(8,128)(2,1)} %get-tuple-element.11) | copy-start | bytes 1572868
  41.5 1.1 %copy-start.1 = (bf16[128,1024]{1,0:T(8,128)(2,1)S(1)}, bf16[128,1024]{1,0:T(8,128)(2,1)}, u32[]{:S(2)}) copy-start(bf16[128,1024]{1,0:T(8,128)(2,1)} %get-tuple-element.12) | copy-start | bytes 786436
  42.5 0.8 %copy-start.2 = (f32[6,16,128]{2,1,0:T(8,128)S(1)}, f32[6,16,128]{2,1,0:T(8,128)}, u32[]{:S(2)}) copy-start(f32[6,16,128]{2,1,0:T(8,128)} %get-tuple-element.13) | copy-start | bytes 147460
  43.3 0.7 %copy-start.3 = (f32[16,128]{1,0:T(8,128)S(1)}, f32[16,128]{1,0:T(8,128)}, u32[]{:S(2)}) copy-start(f32[16,128]{1,0:T(8,128)} %get-tuple-element.14) | copy-start | bytes 24580
where the time goes:
time: 44.9 us; the launch traced here: 44.6 us
  Pallas kernels  38.9 us (87%)
  local copies, waits for them, and re-layouts  5.13 us (11%)
  between operations  0.66 us (1%)
    pallas_call x1, Pallas kernels, shards(): pl.pallas_call(functools.partial(kernel, seq_count, head_count), out_shap...  38.9 us
    unnamed x13, local copies, waits for them, and re-layouts  5.13 us

commit v1 on v0

--- a/solution.py
+++ b/solution.py
@@ -519,6 +519,17 @@
         sq_copy(o, row).wait_send()
 
 
+def write_out(count, *refs):
+    sems = refs[-1]
+    copies = [
+        pltpu.make_async_copy(refs[i], refs[count + i], sems.at[i]) for i in range(count)
+    ]
+    for c in copies:
+        c.start()
+    for c in copies:
+        c.wait()
+
+
 def shards(seq_count, head_count, queries, keys, values, out_grad, log_gate, level_weight, doc_start):
     tok = queries.shape[0]
     heads = log_gate.shape[0]
@@ -574,20 +585,29 @@
         dma((head_count,)),
     ]
     spec = pl.BlockSpec(memory_space=pltpu.VMEM)
-    return pl.pallas_call(
+    outs = [
+        (queries.shape, BF16),
+        (keys.shape, BF16),
+        (values.shape, BF16),
+        (level_weight.shape, F32),
+        (log_gate.shape, F32),
+    ]
+    results = pl.pallas_call(
         functools.partial(kernel, seq_count, head_count),
-        out_shape=(
-            jax.ShapeDtypeStruct(queries.shape, BF16),
-            jax.ShapeDtypeStruct(keys.shape, BF16),
-            jax.ShapeDtypeStruct(values.shape, BF16),
-            jax.ShapeDtypeStruct(level_weight.shape, F32),
-            jax.ShapeDtypeStruct(log_gate.shape, F32),
-        ),
+        out_shape=tuple(vmem(shape, dtype) for shape, dtype in outs),
         in_specs=[spec] * 7,
         out_specs=(spec,) * 5,
         scratch_shapes=scratch,
         compiler_params=pltpu.CompilerParams(collective_id=0, has_side_effects=True),
     )(queries, keys, values, out_grad, log_gate, level_weight, doc_start.reshape(1, tok))
+    count = len(outs)
+    return pl.pallas_call(
+        functools.partial(write_out, count),
+        out_shape=tuple(jax.ShapeDtypeStruct(shape, dtype) for shape, dtype in outs),
+        in_specs=[spec] * count,
+        out_specs=(pl.BlockSpec(memory_space=pltpu.HBM),) * count,
+        scratch_shapes=[dma((count,))],
+    )(*[pltpu.with_memory_space_constraint(r, pltpu.VMEM) for r in results])
 
 
 def solution(mesh):

time: 44.9 us -> 39.7 us (0.88)
  local copies, waits for them, and re-layouts: 5.13 us -> 0 us
    unnamed x13 -> x0, local copies, waits for them, and re-layouts: 5.13 us -> none
    pallas_call x0 -> x1, Pallas kernels: none -> 1.1 us  [shards(): pl.pallas_call(functools.partial(write_out, count), out_shape=tuple((jax....]
    pallas_call x1, Pallas kernels: 38.9 us -> 37.8 us  [shards(): pl.pallas_call(functools.partial(kernel, seq_count, head_count), out_shap...]
where the time goes in v1:
time: 39.7 us; the launch traced here: 39.5 us
  Pallas kernels  38.9 us (98%)
  between operations  0.64 us (2%)
    pallas_call x1, Pallas kernels, shards(): pl.pallas_call(functools.partial(kernel, seq_count, head_count), out_shap...  37.8 us
    pallas_call x1, Pallas kernels, shards(): pl.pallas_call(functools.partial(write_out, count), out_shape=tuple((jax....  1.1 us

profile of v1, /device:TPU:0, one launch (start us, length us, event | category | flops | bytes accessed | tf_op | source)
XLA Modules:
  0.0 39.5 jit_solution(6266901073736883043)
XLA Ops:
  0.6 37.8 %shard_map.110 = (bf16[128,2048]{1,0:T(8,128)(2,1)S(1)}, bf16[128,2048]{1,0:T(8,128)(2,1)S(1)}, bf16[128,1024]{1,0:T(8,128)(2,1)S(1)}, f32[6,16,128]{2,1,0:T(8,128)S(1)}, f32[16,128]{1,0:T(8,128)S(1)}) custom-call(bf16[128,2048]{1,0:T(8,128)(2,1)} %q_ref.1, bf16[128,2048]{1,0:T(8,128)(2,1)} %k_ref.1, bf16[128,1024]{1,0:T(8,128)(2,1)} %v_ref.1, ...), custom_call_target="tpu_custom_call" | custom-call | tf_op jit(solution)/shard_map/pallas_call | solution.py:595
  38.4 1.1 %shard_map.111 = (bf16[128,2048]{1,0:T(8,128)(2,1)}, bf16[128,2048]{1,0:T(8,128)(2,1)}, bf16[128,1024]{1,0:T(8,128)(2,1)}, f32[6,16,128]{2,1,0:T(8,128)}, f32[16,128]{1,0:T(8,128)}) custom-call(bf16[128,2048]{1,0:T(8,128)(2,1)S(1)} %get-tuple-element.10.refs_0_, bf16[128,2048]{1,0:T(8,128)(2,1)S(1)} %get-tuple-element.11.refs_1_, ...), custom_call_target="tpu_custom_call" | custom-call | tf_op jit(solution)/shard_map/pallas_call | solution.py:604

commit v2 on v1

--- a/solution.py
+++ b/solution.py
@@ -519,6 +519,501 @@
         sq_copy(o, row).wait_send()
 
 
+def chunked_kernel(
+    seq_count,
+    head_count,
+    q_ref,
+    k_ref,
+    v_ref,
+    g_ref,
+    lg_ref,
+    lw_ref,
+    ds_ref,
+    gq_ref,
+    gk_ref,
+    gv_ref,
+    gl_ref,
+    gg_ref,
+    cum_s,
+    col_s,
+    lead_s,
+    tail_s,
+    bias_s,
+    vt_s,
+    gt_s,
+    vg_s,
+    gq_s,
+    gk_s,
+    drift_s,
+    coef_s,
+    mix_s,
+    st,
+    got_a,
+    got_b,
+    sum_a,
+    sum_b,
+    sum_q,
+    lvl,
+    decs,
+    tot,
+    sq,
+    a_send,
+    a_recv,
+    b_send,
+    b_recv,
+    p_send,
+    p_recv,
+    xa_send,
+    xa_recv,
+    xb_send,
+    xb_recv,
+    y_send,
+    y_recv,
+    f_send,
+    f_recv,
+    d_send,
+    d_recv,
+    t_send,
+    t_recv,
+    q_send,
+    q_recv,
+):
+    tok = q_ref.shape[0]
+    heads = lg_ref.shape[0]
+    levels = lw_ref.shape[0]
+    dk = q_ref.shape[1] // heads
+    dv = v_ref.shape[1] // heads
+    group = dk // dv
+    pairs = heads // group
+    spans = tok // SPAN
+    span_bits = spans.bit_length() - 1
+    bits = seq_count.bit_length() - 1
+    half = heads // 2
+    chunks = half // group
+    cross = [min(span_bits + 1 + b, levels - 1) for b in range(bits)]
+    slots = sorted(set(cross))
+    kind = [1 + slots.index(l) for l in cross]
+    place = lax.axis_index("seq")
+    row = lax.axis_index("head")
+    core, x, y = [(place // (1 << b)) % 2 for b in range(bits)]
+    peer = [place + (1 - 2 * u) * (1 << b) for b, u in enumerate((core, x, y))]
+    first_chip = (1 - x) * (1 - y)
+    second_chip = x * (1 - y)
+    mine = core * half
+    theirs = (1 - core) * half
+
+    barrier = pltpu.get_barrier_semaphore()
+    for o in range(1, seq_count):
+        pl.semaphore_signal(
+            barrier, inc=1, device_id={"seq": (place + o) % seq_count}, device_id_type=MESH
+        )
+    for o in range(1, head_count):
+        pl.semaphore_signal(
+            barrier, inc=1, device_id={"head": (row + o) % head_count}, device_id_type=MESH
+        )
+
+    rows_i = lax.broadcasted_iota(jnp.int32, (tok, tok), 0)
+    cols_i = lax.broadcasted_iota(jnp.int32, (tok, tok), 1)
+    tri = (rows_i <= cols_i).astype(F32)
+    starts = jnp.broadcast_to(ds_ref[...].astype(F32), (8, tok))
+    both = jnp.concatenate([lg_ref[...], starts], axis=0)
+    cum_all = lax.dot_general(
+        both, tri, NN, precision=lax.Precision.HIGHEST, preferred_element_type=F32
+    )
+    cum_t = jnp.transpose(
+        jnp.concatenate([cum_all, jnp.zeros((dk - heads - 8, tok), F32)], axis=0)
+    )
+    cum = cum_all[:heads]
+    reset = cum_all[heads : heads + 1]
+    reset_col = cum_t[:, heads : heads + 1]
+    bias_s[...] = jnp.where((rows_i <= cols_i) & (reset == reset_col), 0.0, -1e30)
+    end = cum[:, tok - 1 : tok]
+    reset_end = reset[:, tok - 1 : tok]
+    cum_s[...] = cum
+    lead_s[...] = jnp.where(reset == 0, jnp.exp(cum), 0.0)
+    tail_s[...] = jnp.where(reset == reset_end, jnp.exp(end - cum), 0.0)
+    lane_row = lax.broadcasted_iota(jnp.int32, (1, dk), 1)
+    end_row = jnp.where(lane_row < heads, cum_t[tok - 1 : tok, :], 0.0)
+    decs[place] = jnp.where(reset_end == 0, jnp.exp(end_row), 0.0)
+    for h in range(heads):
+        col_s[h] = jnp.broadcast_to(cum_t[:, h : h + 1], (tok, tok))
+
+    def states(p, _):
+        lanes = pl.ds(pl.multiple_of(p * dk, dk), dk)
+        vt = jnp.transpose(v_ref[:, lanes].astype(F32))
+        gt = jnp.transpose(g_ref[:, lanes].astype(F32))
+        vt_s[p] = vt.astype(BF16)
+        gt_s[p] = gt.astype(BF16)
+        for i in range(group):
+            h = p * group + i
+            wide = pl.ds(pl.multiple_of(h * dk, dk), dk)
+            part = slice(i * dv, (i + 1) * dv)
+            tail = tail_s[pl.ds(h, 1), :]
+            lead = lead_s[pl.ds(h, 1), :]
+            st[0, h] = dot_fine(vt[part] * tail, k_ref[:, wide], NN)
+            gw = jnp.concatenate(
+                [gt[part] * (lead * lw_ref[l, pl.ds(h, 1), :]) for l in slots], axis=0
+            )
+            back = dot_fine(gw, q_ref[:, wide], NN)
+            for n in range(len(slots)):
+                st[1 + n, h] = back[n * dv : (n + 1) * dv]
+        return 0
+
+    lax.fori_loop(0, pairs, states, 0, unroll=2)
+    pl.semaphore_wait(barrier, seq_count - 1 + head_count - 1)
+
+    def remote(src, dst, send, recv, b):
+        return pltpu.make_async_remote_copy(
+            src_ref=src,
+            dst_ref=dst,
+            send_sem=send,
+            recv_sem=recv,
+            device_id={"seq": peer[b]},
+            device_id_type=MESH,
+        )
+
+    def of(base, c):
+        return pl.ds(base + c * group, group)
+
+    def at(c):
+        return pl.ds(c * group, group)
+
+    kind_a = y * kind[2]
+    kind_b = x * kind[1]
+    slot_out = bits - (bits - 1) * first_chip
+    slot_in = bits - (bits - 1) * second_chip
+
+    def dec_copy(o, slot_at):
+        return pltpu.make_async_remote_copy(
+            src_ref=decs.at[place],
+            dst_ref=decs.at[slot_at],
+            send_sem=d_send.at[o],
+            recv_sem=d_recv.at[slot_at],
+            device_id={"seq": (place + o) % seq_count},
+            device_id_type=MESH,
+        )
+
+    def a_copy(c):
+        return remote(
+            st.at[kind_a, of(theirs, c)], got_a.at[at(c)], a_send.at[c], a_recv.at[c], 0
+        )
+
+    def b_copy(c):
+        return remote(
+            st.at[kind_b, of(theirs, c)], got_b.at[at(c)], b_send.at[c], b_recv.at[c], 0
+        )
+
+    def p_copy():
+        return remote(st.at[core * kind[0]], lvl.at[0], p_send.at[0], p_recv.at[0], 0)
+
+    def xa_copy(c):
+        return remote(
+            sum_a.at[at(c)], lvl.at[slot_out, of(mine, c)], xa_send.at[c], xa_recv.at[c], 1
+        )
+
+    def xb_copy(c):
+        return remote(sum_b.at[at(c)], lvl.at[1, of(mine, c)], xb_send.at[c], xb_recv.at[c], 1)
+
+    def y_copy(c):
+        return remote(sum_q.at[at(c)], lvl.at[2, of(mine, c)], y_send.at[c], y_recv.at[c], 2)
+
+    def f_copy(j, base, c):
+        part = lvl.at[j, of(base, c)]
+        return remote(part, part, f_send.at[j - 1, c], f_recv.at[j - 1, c], 0)
+
+    for o in range(1, seq_count):
+        dec_copy(o, place).start()
+    for c in range(chunks):
+        a_copy(c).start()
+
+    @pl.when(first_chip == 0)
+    def _():
+        for c in range(chunks):
+            b_copy(c).start()
+
+    p_copy().start()
+
+    span_of = lax.broadcasted_iota(jnp.int32, (1, tok), 1) // SPAN
+
+    def local(p, _):
+        vt = vt_s[p]
+        gt = gt_s[p]
+        lanes = pl.ds(pl.multiple_of(p * dk, dk), dk)
+        v_blk = v_ref[:, lanes]
+        for i in range(group):
+            h = p * group + i
+            wide = pl.ds(pl.multiple_of(h * dk, dk), dk)
+            part = slice(i * dv, (i + 1) * dv)
+            q = q_ref[:, wide]
+            k = k_ref[:, wide]
+            score = dot(k, q, NT)
+            pair = dot(v_blk[:, part], gt[part], NN)
+            decay = jnp.exp((cum_s[pl.ds(h, 1), :] - col_s[h]) + bias_s[...])
+            seen = decay * score
+            both_p = seen * pair
+            gains = [lw_ref[l, pl.ds(h, 1), :] for l in range(span_bits + 1)]
+            level_rows = [jnp.zeros((1, tok), F32) for _ in range(span_bits + 1)]
+            mixed, graded = [], []
+            for cs in range(spans):
+                rows = slice(cs * SPAN, (cs + 1) * SPAN)
+                total = jnp.sum(both_p[rows], axis=0, keepdims=True)
+                gain = jnp.zeros((1, tok), F32)
+                for ct in range(cs, spans):
+                    l = span_level(cs, ct, levels)
+                    hit = span_of == ct
+                    gain = jnp.where(hit, gains[l], gain)
+                    level_rows[l] = level_rows[l] + jnp.where(hit, total, 0.0)
+                mixed.append(seen[rows] * gain)
+                graded.append(decay[rows] * gain * pair[rows])
+            mix = jnp.concatenate(mixed, axis=0).astype(BF16)
+            grade = jnp.concatenate(graded, axis=0).astype(BF16)
+            for l in range(span_bits + 1):
+                gl_ref[l, pl.ds(h, 1), :] = level_rows[l]
+            drift_s[pl.ds(h, 1), :] = jnp.sum(mix.astype(F32) * pair, axis=0, keepdims=True)
+            vg_s[p, part] = dot(gt[part], mix, NT)
+            gk_s[h] = dot(grade, q, NN)
+            gq_s[h] = dot(grade, k, TN)
+        return 0
+
+    def decay_of(device):
+        return decs[device]
+
+    def wait_dec(device):
+        dec_copy((device + seq_count - place) % seq_count, device).wait_recv()
+
+    def spread(device_rows):
+        t = jnp.transpose(
+            jnp.concatenate(
+                device_rows + [jnp.zeros((8 - len(device_rows), dk), F32)], axis=0
+            )
+        )
+        return [
+            jnp.broadcast_to(t[:heads, n : n + 1], (heads, dk)) for n in range(len(device_rows))
+        ]
+
+    def weigh(n, swap, own, got):
+        w = (swap % 2).astype(F32)
+        mix_s[n, 0] = own * (1.0 - w) + w
+        mix_s[n, 1] = got * w + (1.0 - w)
+
+    def combine(n, c, own_at, got_at, put):
+        for i in range(group):
+            r = c * group + i
+            ca = mix_s[n, 0, pl.ds(mine + r, 1), :]
+            cb = mix_s[n, 1, pl.ds(mine + r, 1), :]
+            put[r] = ca * own_at(r) + cb * got_at(r)
+
+    lax.fori_loop(0, 2, local, 0, unroll=2)
+
+    dec_recv = [peer[0], peer[1], peer[1] + 1 - 2 * core]
+    wait_dec(dec_recv[0])
+    d_self, d_pair = spread([decay_of(place), decay_of(dec_recv[0])])
+    weigh(0, core + y, d_pair, d_self)
+    weigh(1, core + x, d_pair, d_self)
+    for c in range(chunks):
+        a_copy(c).wait_recv()
+        combine(0, c, lambda r: st[kind_a, mine + r], lambda r: got_a[r], sum_a)
+        xa_copy(c).start()
+
+    @pl.when(first_chip == 0)
+    def _():
+        for c in range(chunks):
+            b_copy(c).wait_recv()
+            combine(1, c, lambda r: st[kind_b, mine + r], lambda r: got_b[r], sum_b)
+            xb_copy(c).start()
+
+    lax.fori_loop(2, pairs - 2, local, 0, unroll=2)
+
+    for n in (1, 2):
+        wait_dec(dec_recv[n])
+    side, other_side = spread([decay_of(dec_recv[1]), decay_of(dec_recv[2])])
+    d_side = side * other_side
+    weigh(2, x + y, d_side, d_self * d_pair)
+    inner_f = jnp.ones((heads, dk), F32)
+    inner_b = jnp.ones((heads, dk), F32)
+    for b, (u, got) in enumerate(((core, d_pair), (x, d_side), (y, None))):
+        up = u.astype(F32)
+        coef_s[0, b] = inner_f * up
+        coef_s[1, b] = inner_b * (1.0 - up)
+        if got is not None:
+            inner_f = inner_f * (up * got + (1.0 - up))
+            inner_b = inner_b * ((1.0 - up) * got + up)
+
+    for c in range(chunks):
+        xa_copy(c).wait_recv()
+        combine(2, c, lambda r: sum_a[r], lambda r: lvl[slot_in, mine + r], sum_q)
+        y_copy(c).start()
+
+        @pl.when(second_chip == 1)
+        def _(c=c):
+            f_copy(1, mine, c).start()
+
+        if c == 0:
+            lax.fori_loop(pairs - 2, pairs, local, 0, unroll=2)
+
+    def finish(p, _):
+        lanes = pl.ds(pl.multiple_of(p * dk, dk), dk)
+        vt = vt_s[p].astype(F32)
+        gt = gt_s[p].astype(F32)
+        vg_all = []
+        for i in range(group):
+            h = p * group + i
+            wide = pl.ds(pl.multiple_of(h * dk, dk), dk)
+            part = slice(i * dv, (i + 1) * dv)
+            q = q_ref[:, wide]
+            k = k_ref[:, wide]
+            tail = tail_s[pl.ds(h, 1), :]
+            lead = lead_s[pl.ds(h, 1), :]
+            blocks = [lvl[b, h] for b in range(bits)]
+            entering = []
+            for n in range(len(slots)):
+                terms = [
+                    coef_s[0, b, pl.ds(h, 1), :] * blocks[b]
+                    for b in range(bits)
+                    if kind[b] == 1 + n
+                ]
+                entering.append(functools.reduce(jnp.add, terms))
+            entering = jnp.concatenate(entering, axis=0)
+            after = functools.reduce(
+                jnp.add, [coef_s[1, b, pl.ds(h, 1), :] * blocks[b] for b in range(bits)]
+            )
+            e_high, e_low = split(entering)
+            seen = dot(e_high, q, NT) + dot(e_low, q, NT)
+            drift = drift_s[pl.ds(h, 1), :]
+            gws = []
+            for n, l in enumerate(slots):
+                gain = lw_ref[l, pl.ds(h, 1), :]
+                level = lead * jnp.sum(
+                    seen[n * dv : (n + 1) * dv] * gt[part], axis=0, keepdims=True
+                )
+                gl_ref[l, pl.ds(h, 1), :] = level
+                drift = drift + gain * level
+                gws.append(gt[part] * (lead * gain))
+            gw, gw_low = split(jnp.concatenate(gws, axis=0))
+            gq_in = dot(gw, e_high, TN) + dot(gw, e_low, TN) + dot(gw_low, e_high, TN)
+            gq_ref[:, wide] = (gq_s[h] + gq_in).astype(BF16)
+            a_high, a_low = split(after)
+            tv, tv_low = split(vt[part] * tail)
+            gk_in = dot(tv, a_high, TN) + dot(tv, a_low, TN) + dot(tv_low, a_high, TN)
+            gk_ref[:, wide] = (gk_s[h] + gk_in).astype(BF16)
+            vg = vg_s[p, part] + tail * (dot(a_high, k, NT) + dot(a_low, k, NT))
+            drift_s[pl.ds(h, 1), :] = drift - jnp.sum(vg * vt[part], axis=0, keepdims=True)
+            vg_all.append(vg)
+        gv_ref[:, lanes] = jnp.transpose(jnp.concatenate(vg_all, axis=0)).astype(BF16)
+        return 0
+
+    def finish_chunk(c):
+        if c == 0:
+            p_copy().wait_recv()
+        for j in (1, 2):
+            f_copy(j, theirs, c).wait_recv()
+        lax.fori_loop(0, 2, lambda i, _: finish(c + i * chunks, 0), 0, unroll=2)
+
+    for c in range(chunks):
+
+        @pl.when(second_chip == 0)
+        def _(c=c):
+            xb_copy(c).wait_recv()
+            f_copy(1, mine, c).start()
+
+        y_copy(c).wait_recv()
+        f_copy(2, mine, c).start()
+        if c > 0:
+            finish_chunk(c - 1)
+    finish_chunk(chunks - 1)
+    for l in range(levels):
+        if l > span_bits and l not in slots:
+            gl_ref[l] = jnp.zeros((heads, tok), F32)
+
+    later = (rows_i >= cols_i).astype(F32)
+    local_tail = lax.dot_general(
+        drift_s[...], later, NN, precision=lax.Precision.HIGHEST, preferred_element_type=F32
+    )
+    lane = lax.broadcasted_iota(jnp.int32, (heads, tok), 1)
+    first = local_tail[:, 0:1]
+    plain = jnp.sum(local_tail, axis=1, keepdims=True)
+    square = jnp.sum(local_tail * local_tail, axis=1, keepdims=True)
+    tot[place] = jnp.where(lane == 0, first, jnp.where(lane == 1, plain, square))
+
+    def tot_copy(o, slot_at):
+        return pltpu.make_async_remote_copy(
+            src_ref=tot.at[place],
+            dst_ref=tot.at[slot_at],
+            send_sem=t_send.at[o],
+            recv_sem=t_recv.at[slot_at],
+            device_id={"seq": (place + o) % seq_count},
+            device_id_type=MESH,
+        )
+
+    for o in range(1, seq_count):
+        tot_copy(o, place).start()
+    for o in range(1, seq_count):
+        tot_copy(o, (place + o) % seq_count).wait_recv()
+    after_total = jnp.zeros((heads, 1), F32)
+    my_later = jnp.zeros((heads, 1), F32)
+    energy = jnp.zeros((heads, 1), F32)
+    for d in reversed(range(seq_count)):
+        piece = tot[d]
+        my_later = my_later + jnp.where(place == d, 1.0, 0.0) * after_total
+        energy = energy + (
+            piece[:, 2:3] + after_total * (2.0 * piece[:, 1:2] + tok * after_total)
+        )
+        after_total = after_total + piece[:, 0:1]
+    energy = jnp.sum(jnp.broadcast_to(energy, (heads, dk)), axis=0, keepdims=True)
+    sq[row] = jnp.broadcast_to(energy, (8, dk))
+
+    def sq_copy(o, slot_at):
+        return pltpu.make_async_remote_copy(
+            src_ref=sq.at[row],
+            dst_ref=sq.at[slot_at],
+            send_sem=q_send.at[o],
+            recv_sem=q_recv.at[slot_at],
+            device_id={"head": (row + o) % head_count},
+            device_id_type=MESH,
+        )
+
+    for o in range(1, head_count):
+        sq_copy(o, row).start()
+    for o in range(1, head_count):
+        sq_copy(o, (row + o) % head_count).wait_recv()
+    whole = sq[0]
+    for r in range(1, head_count):
+        whole = whole + sq[r]
+    count = heads * tok * seq_count * head_count
+    factor = jnp.minimum(1.0, lax.rsqrt(whole[0:1] / count + 1e-6))
+    gg_ref[...] = (local_tail + my_later) * factor
+
+    for o in range(1, seq_count):
+        dec_copy(o, place).wait_send()
+
+        @pl.when((place + o) % seq_count != dec_recv[0])
+        def _(o=o):
+            device = (place + o) % seq_count
+
+            @pl.when((device != dec_recv[1]) & (device != dec_recv[2]))
+            def _():
+                wait_dec(device)
+
+    p_copy().wait_send()
+    for c in range(chunks):
+        a_copy(c).wait_send()
+        xa_copy(c).wait_send()
+        y_copy(c).wait_send()
+        for j in (1, 2):
+            f_copy(j, mine, c).wait_send()
+
+    @pl.when(first_chip == 0)
+    def _():
+        for c in range(chunks):
+            b_copy(c).wait_send()
+            xb_copy(c).wait_send()
+
+    for o in range(1, seq_count):
+        tot_copy(o, place).wait_send()
+    for o in range(1, head_count):
+        sq_copy(o, row).wait_send()
+
+
 def write_out(count, *refs):
     sems = refs[-1]
     copies = [
@@ -584,6 +1079,43 @@
         dma((head_count,)),
         dma((head_count,)),
     ]
+    body = kernel
+    chunks = half // group
+    if bits == 3 and chunks * group == half:
+        body = chunked_kernel
+        scratch = scratch[:12] + [
+            vmem((3, 2, heads, dk), F32),
+            vmem((1 + slots, heads) + block, F32),
+            vmem((half,) + block, F32),
+            vmem((half,) + block, F32),
+            vmem((half,) + block, F32),
+            vmem((half,) + block, F32),
+            vmem((half,) + block, F32),
+            vmem((bits + 1, heads) + block, F32),
+            vmem((seq_count, 1, dk), F32),
+            vmem((seq_count, heads, tok), F32),
+            vmem((head_count, 8, dk), F32),
+            dma((chunks,)),
+            dma((chunks,)),
+            dma((chunks,)),
+            dma((chunks,)),
+            dma((1,)),
+            dma((1,)),
+            dma((chunks,)),
+            dma((chunks,)),
+            dma((chunks,)),
+            dma((chunks,)),
+            dma((chunks,)),
+            dma((chunks,)),
+            dma((2, chunks)),
+            dma((2, chunks)),
+            dma((seq_count,)),
+            dma((seq_count,)),
+            dma((seq_count,)),
+            dma((seq_count,)),
+            dma((head_count,)),
+            dma((head_count,)),
+        ]
     spec = pl.BlockSpec(memory_space=pltpu.VMEM)
     outs = [
         (queries.shape, BF16),
@@ -593,7 +1125,7 @@
         (log_gate.shape, F32),
     ]
     results = pl.pallas_call(
-        functools.partial(kernel, seq_count, head_count),
+        functools.partial(body, seq_count, head_count),
         out_shape=tuple(vmem(shape, dtype) for shape, dtype in outs),
         in_specs=[spec] * 7,
         out_specs=(spec,) * 5,

time: 39.7 us -> 33.8 us (0.85)
  Pallas kernels: 38.9 us -> 33 us
    pallas_call x1, Pallas kernels: 37.8 us -> 31.9 us  [shards(): pl.pallas_call(functools.partial(body, seq_count, head_count), out_shape=...]
where the time goes in v2:
time: 33.8 us; the launch traced here: 33.6 us
  Pallas kernels  33 us (98%)
  between operations  0.64 us (2%)
    pallas_call x1, Pallas kernels, shards(): pl.pallas_call(functools.partial(body, seq_count, head_count), out_shape=...  31.9 us
    pallas_call x1, Pallas kernels, shards(): pl.pallas_call(functools.partial(write_out, count), out_shape=tuple((jax....  1.1 us

profile of v2, /device:TPU:0, one launch (start us, length us, event | category | flops | bytes accessed | tf_op | source)
XLA Modules:
  0.0 33.6 jit_solution(17130256141510015676)
XLA Ops:
  0.6 31.9 %shard_map.110 = (bf16[128,2048]{1,0:T(8,128)(2,1)S(1)}, bf16[128,2048]{1,0:T(8,128)(2,1)S(1)}, bf16[128,1024]{1,0:T(8,128)(2,1)S(1)}, f32[6,16,128]{2,1,0:T(8,128)S(1)}, f32[16,128]{1,0:T(8,128)S(1)}) custom-call(bf16[128,2048]{1,0:T(8,128)(2,1)} %q_ref.1, bf16[128,2048]{1,0:T(8,128)(2,1)} %k_ref.1, bf16[128,1024]{1,0:T(8,128)(2,1)} %v_ref.1, ...), custom_call_target="tpu_custom_call" | custom-call | tf_op jit(solution)/shard_map/pallas_call | solution.py:1127
  32.5 1.1 %shard_map.111 = (bf16[128,2048]{1,0:T(8,128)(2,1)}, bf16[128,2048]{1,0:T(8,128)(2,1)}, bf16[128,1024]{1,0:T(8,128)(2,1)}, f32[6,16,128]{2,1,0:T(8,128)}, f32[16,128]{1,0:T(8,128)}) custom-call(bf16[128,2048]{1,0:T(8,128)(2,1)S(1)} %get-tuple-element.10.refs_0_, bf16[128,2048]{1,0:T(8,128)(2,1)S(1)} %get-tuple-element.11.refs_1_, ...), custom_call_target="tpu_custom_call" | custom-call | tf_op jit(solution)/shard_map/pallas_call | solution.py:1136

commit v3 on v2

--- a/solution.py
+++ b/solution.py
@@ -522,6 +522,18 @@
 def chunked_kernel(
     seq_count,
     head_count,
+    q_hbm,
+    k_hbm,
+    v_hbm,
+    g_hbm,
+    lg_hbm,
+    lw_hbm,
+    ds_hbm,
+    gq_ref,
+    gk_ref,
+    gv_ref,
+    gl_ref,
+    gg_ref,
     q_ref,
     k_ref,
     v_ref,
@@ -529,11 +541,6 @@
     lg_ref,
     lw_ref,
     ds_ref,
-    gq_ref,
-    gk_ref,
-    gv_ref,
-    gl_ref,
-    gg_ref,
     cum_s,
     col_s,
     lead_s,
@@ -555,8 +562,8 @@
     sum_q,
     lvl,
     decs,
-    tot,
-    sq,
+    msg,
+    i_sem,
     a_send,
     a_recv,
     b_send,
@@ -575,8 +582,8 @@
     d_recv,
     t_send,
     t_recv,
-    q_send,
-    q_recv,
+    round_sem,
+    plane_sem,
 ):
     tok = q_ref.shape[0]
     heads = lg_ref.shape[0]
@@ -602,15 +609,32 @@
     mine = core * half
     theirs = (1 - core) * half
 
+    has_next = (row < head_count - 1).astype(jnp.int32)
+    has_last = (row > 0).astype(jnp.int32)
+
+    def greet(sem):
+        @pl.when(has_next == 1)
+        def _():
+            pl.semaphore_signal(sem, inc=1, device_id={"head": row + 1}, device_id_type=MESH)
+
+        @pl.when(has_last == 1)
+        def _():
+            pl.semaphore_signal(sem, inc=1, device_id={"head": row - 1}, device_id_type=MESH)
+
     barrier = pltpu.get_barrier_semaphore()
-    for o in range(1, seq_count):
-        pl.semaphore_signal(
-            barrier, inc=1, device_id={"seq": (place + o) % seq_count}, device_id_type=MESH
-        )
-    for o in range(1, head_count):
-        pl.semaphore_signal(
-            barrier, inc=1, device_id={"head": (row + o) % head_count}, device_id_type=MESH
-        )
+    for b in reversed(range(bits)):
+        pl.semaphore_signal(barrier, inc=1, device_id={"seq": peer[b]}, device_id_type=MESH)
+    greet(barrier)
+
+    def load(n):
+        src = (lg_hbm, ds_hbm, v_hbm, k_hbm, g_hbm, lw_hbm, q_hbm)[n]
+        dst = (lg_ref, ds_ref, v_ref, k_ref, g_ref, lw_ref, q_ref)[n]
+        return pltpu.make_async_copy(src, dst, i_sem.at[n])
+
+    for n in range(7):
+        load(n).start()
+    for n in range(2):
+        load(n).wait()
 
     rows_i = lax.broadcasted_iota(jnp.int32, (tok, tok), 0)
     cols_i = lax.broadcasted_iota(jnp.int32, (tok, tok), 1)
@@ -634,7 +658,7 @@
     tail_s[...] = jnp.where(reset == reset_end, jnp.exp(end - cum), 0.0)
     lane_row = lax.broadcasted_iota(jnp.int32, (1, dk), 1)
     end_row = jnp.where(lane_row < heads, cum_t[tok - 1 : tok, :], 0.0)
-    decs[place] = jnp.where(reset_end == 0, jnp.exp(end_row), 0.0)
+    decs[0] = jnp.where(reset_end == 0, jnp.exp(end_row), 0.0)
     for h in range(heads):
         col_s[h] = jnp.broadcast_to(cum_t[:, h : h + 1], (tok, tok))
 
@@ -659,8 +683,13 @@
                 st[1 + n, h] = back[n * dv : (n + 1) * dv]
         return 0
 
+    for n in range(2, 7):
+        load(n).wait()
     lax.fori_loop(0, pairs, states, 0, unroll=2)
-    pl.semaphore_wait(barrier, seq_count - 1 + head_count - 1)
+    pl.semaphore_wait(barrier, bits + has_next + has_last)
+    rounds = head_count - 2
+    if rounds > 0:
+        greet(round_sem.at[0])
 
     def remote(src, dst, send, recv, b):
         return pltpu.make_async_remote_copy(
@@ -683,15 +712,8 @@
     slot_out = bits - (bits - 1) * first_chip
     slot_in = bits - (bits - 1) * second_chip
 
-    def dec_copy(o, slot_at):
-        return pltpu.make_async_remote_copy(
-            src_ref=decs.at[place],
-            dst_ref=decs.at[slot_at],
-            send_sem=d_send.at[o],
-            recv_sem=d_recv.at[slot_at],
-            device_id={"seq": (place + o) % seq_count},
-            device_id_type=MESH,
-        )
+    def dec_copy(n):
+        return remote(decs.at[2 * n], decs.at[2 * n + 1], d_send.at[n], d_recv.at[n], n)
 
     def a_copy(c):
         return remote(
@@ -721,8 +743,7 @@
         part = lvl.at[j, of(base, c)]
         return remote(part, part, f_send.at[j - 1, c], f_recv.at[j - 1, c], 0)
 
-    for o in range(1, seq_count):
-        dec_copy(o, place).start()
+    dec_copy(0).start()
     for c in range(chunks):
         a_copy(c).start()
 
@@ -775,12 +796,6 @@
             gq_s[h] = dot(grade, k, TN)
         return 0
 
-    def decay_of(device):
-        return decs[device]
-
-    def wait_dec(device):
-        dec_copy((device + seq_count - place) % seq_count, device).wait_recv()
-
     def spread(device_rows):
         t = jnp.transpose(
             jnp.concatenate(
@@ -805,9 +820,9 @@
 
     lax.fori_loop(0, 2, local, 0, unroll=2)
 
-    dec_recv = [peer[0], peer[1], peer[1] + 1 - 2 * core]
-    wait_dec(dec_recv[0])
-    d_self, d_pair = spread([decay_of(place), decay_of(dec_recv[0])])
+    dec_copy(0).wait_recv()
+    decs[2] = decs[0] * decs[1]
+    d_self, d_pair = spread([decs[0], decs[1]])
     weigh(0, core + y, d_pair, d_self)
     weigh(1, core + x, d_pair, d_self)
     for c in range(chunks):
@@ -815,6 +830,8 @@
         combine(0, c, lambda r: st[kind_a, mine + r], lambda r: got_a[r], sum_a)
         xa_copy(c).start()
 
+    dec_copy(1).start()
+
     @pl.when(first_chip == 0)
     def _():
         for c in range(chunks):
@@ -824,10 +841,12 @@
 
     lax.fori_loop(2, pairs - 2, local, 0, unroll=2)
 
-    for n in (1, 2):
-        wait_dec(dec_recv[n])
-    side, other_side = spread([decay_of(dec_recv[1]), decay_of(dec_recv[2])])
-    d_side = side * other_side
+    for r in range(1, rounds + 1):
+        pl.semaphore_wait(round_sem.at[r - 1], has_next + has_last)
+        if r < rounds:
+            greet(round_sem.at[r])
+    dec_copy(1).wait_recv()
+    (d_side,) = spread([decs[3]])
     weigh(2, x + y, d_side, d_self * d_pair)
     inner_f = jnp.ones((heads, dk), F32)
     inner_b = jnp.ones((heads, dk), F32)
@@ -851,11 +870,24 @@
         if c == 0:
             lax.fori_loop(pairs - 2, pairs, local, 0, unroll=2)
 
-    def finish(p, _):
-        lanes = pl.ds(pl.multiple_of(p * dk, dk), dk)
+    def incoming(h):
+        blocks = [lvl[b, h] for b in range(bits)]
+        entering = []
+        for n in range(len(slots)):
+            terms = [
+                coef_s[0, b, pl.ds(h, 1), :] * blocks[b]
+                for b in range(bits)
+                if kind[b] == 1 + n
+            ]
+            entering.append(functools.reduce(jnp.add, terms))
+        after = functools.reduce(
+            jnp.add, [coef_s[1, b, pl.ds(h, 1), :] * blocks[b] for b in range(bits)]
+        )
+        return split(jnp.concatenate(entering, axis=0)), split(after)
+
+    def finish_drift(p):
         vt = vt_s[p].astype(F32)
         gt = gt_s[p].astype(F32)
-        vg_all = []
         for i in range(group):
             h = p * group + i
             wide = pl.ds(pl.multiple_of(h * dk, dk), dk)
@@ -864,51 +896,42 @@
             k = k_ref[:, wide]
             tail = tail_s[pl.ds(h, 1), :]
             lead = lead_s[pl.ds(h, 1), :]
-            blocks = [lvl[b, h] for b in range(bits)]
-            entering = []
-            for n in range(len(slots)):
-                terms = [
-                    coef_s[0, b, pl.ds(h, 1), :] * blocks[b]
-                    for b in range(bits)
-                    if kind[b] == 1 + n
-                ]
-                entering.append(functools.reduce(jnp.add, terms))
-            entering = jnp.concatenate(entering, axis=0)
-            after = functools.reduce(
-                jnp.add, [coef_s[1, b, pl.ds(h, 1), :] * blocks[b] for b in range(bits)]
-            )
-            e_high, e_low = split(entering)
+            (e_high, e_low), (a_high, a_low) = incoming(h)
             seen = dot(e_high, q, NT) + dot(e_low, q, NT)
             drift = drift_s[pl.ds(h, 1), :]
-            gws = []
             for n, l in enumerate(slots):
-                gain = lw_ref[l, pl.ds(h, 1), :]
                 level = lead * jnp.sum(
                     seen[n * dv : (n + 1) * dv] * gt[part], axis=0, keepdims=True
                 )
                 gl_ref[l, pl.ds(h, 1), :] = level
-                drift = drift + gain * level
-                gws.append(gt[part] * (lead * gain))
+                drift = drift + lw_ref[l, pl.ds(h, 1), :] * level
+            vg = vg_s[p, part] + tail * (dot(a_high, k, NT) + dot(a_low, k, NT))
+            drift_s[pl.ds(h, 1), :] = drift - jnp.sum(vg * vt[part], axis=0, keepdims=True)
+            vg_s[p, part] = vg
+
+    def finish_out(p):
+        lanes = pl.ds(pl.multiple_of(p * dk, dk), dk)
+        vt = vt_s[p].astype(F32)
+        gt = gt_s[p].astype(F32)
+        for i in range(group):
+            h = p * group + i
+            wide = pl.ds(pl.multiple_of(h * dk, dk), dk)
+            part = slice(i * dv, (i + 1) * dv)
+            tail = tail_s[pl.ds(h, 1), :]
+            lead = lead_s[pl.ds(h, 1), :]
+            (e_high, e_low), (a_high, a_low) = incoming(h)
+            gws = [gt[part] * (lead * lw_ref[l, pl.ds(h, 1), :]) for l in slots]
             gw, gw_low = split(jnp.concatenate(gws, axis=0))
             gq_in = dot(gw, e_high, TN) + dot(gw, e_low, TN) + dot(gw_low, e_high, TN)
             gq_ref[:, wide] = (gq_s[h] + gq_in).astype(BF16)
-            a_high, a_low = split(after)
             tv, tv_low = split(vt[part] * tail)
             gk_in = dot(tv, a_high, TN) + dot(tv, a_low, TN) + dot(tv_low, a_high, TN)
             gk_ref[:, wide] = (gk_s[h] + gk_in).astype(BF16)
-            vg = vg_s[p, part] + tail * (dot(a_high, k, NT) + dot(a_low, k, NT))
-            drift_s[pl.ds(h, 1), :] = drift - jnp.sum(vg * vt[part], axis=0, keepdims=True)
-            vg_all.append(vg)
-        gv_ref[:, lanes] = jnp.transpose(jnp.concatenate(vg_all, axis=0)).astype(BF16)
-        return 0
-
-    def finish_chunk(c):
-        if c == 0:
-            p_copy().wait_recv()
-        for j in (1, 2):
-            f_copy(j, theirs, c).wait_recv()
-        lax.fori_loop(0, 2, lambda i, _: finish(c + i * chunks, 0), 0, unroll=2)
-
+        gv_ref[:, lanes] = jnp.transpose(vg_s[p]).astype(BF16)
+
+    own_pair = core * chunks
+    far_pair = (1 - core) * chunks
+    p_copy().wait_recv()
     for c in range(chunks):
 
         @pl.when(second_chip == 0)
@@ -918,82 +941,76 @@
 
         y_copy(c).wait_recv()
         f_copy(2, mine, c).start()
-        if c > 0:
-            finish_chunk(c - 1)
-    finish_chunk(chunks - 1)
-    for l in range(levels):
-        if l > span_bits and l not in slots:
-            gl_ref[l] = jnp.zeros((heads, tok), F32)
+        if c == 0:
+            for o in range(1, head_count):
+                pl.semaphore_signal(
+                    plane_sem,
+                    inc=1,
+                    device_id={"head": (row + o) % head_count},
+                    device_id_type=MESH,
+                )
+        finish_drift(own_pair + c)
+        if c < chunks - 1:
+            finish_out(own_pair + c)
+        for j in (1, 2):
+            f_copy(j, theirs, c).wait_recv()
+        finish_drift(far_pair + c)
+        if c < chunks - 1:
+            finish_out(far_pair + c)
 
     later = (rows_i >= cols_i).astype(F32)
     local_tail = lax.dot_general(
         drift_s[...], later, NN, precision=lax.Precision.HIGHEST, preferred_element_type=F32
     )
     lane = lax.broadcasted_iota(jnp.int32, (heads, tok), 1)
-    first = local_tail[:, 0:1]
-    plain = jnp.sum(local_tail, axis=1, keepdims=True)
-    square = jnp.sum(local_tail * local_tail, axis=1, keepdims=True)
-    tot[place] = jnp.where(lane == 0, first, jnp.where(lane == 1, plain, square))
-
-    def tot_copy(o, slot_at):
+    head = lax.broadcasted_iota(jnp.int32, (heads, tok), 0)
+    sums = [
+        local_tail[:, 0:1],
+        jnp.sum(local_tail, axis=1, keepdims=True),
+        jnp.sum(local_tail * local_tail, axis=1, keepdims=True),
+    ]
+    packed = jnp.zeros((heads, tok), F32)
+    for n, column in enumerate(sums):
+        packed = jnp.where(lane == head + n * heads, column, packed)
+    slot = row * seq_count + place
+    total = seq_count * head_count
+    msg[slot] = jnp.sum(packed, axis=0, keepdims=True)
+
+    def tail_copy(to_row, to_place):
         return pltpu.make_async_remote_copy(
-            src_ref=tot.at[place],
-            dst_ref=tot.at[slot_at],
-            send_sem=t_send.at[o],
-            recv_sem=t_recv.at[slot_at],
-            device_id={"seq": (place + o) % seq_count},
+            src_ref=msg.at[slot],
+            dst_ref=msg.at[slot],
+            send_sem=t_send.at[0],
+            recv_sem=t_recv.at[0],
+            device_id={"seq": to_place, "head": to_row},
             device_id_type=MESH,
         )
 
-    for o in range(1, seq_count):
-        tot_copy(o, place).start()
-    for o in range(1, seq_count):
-        tot_copy(o, (place + o) % seq_count).wait_recv()
-    after_total = jnp.zeros((heads, 1), F32)
-    my_later = jnp.zeros((heads, 1), F32)
-    energy = jnp.zeros((heads, 1), F32)
-    for d in reversed(range(seq_count)):
-        piece = tot[d]
-        my_later = my_later + jnp.where(place == d, 1.0, 0.0) * after_total
-        energy = energy + (
-            piece[:, 2:3] + after_total * (2.0 * piece[:, 1:2] + tok * after_total)
-        )
-        after_total = after_total + piece[:, 0:1]
-    energy = jnp.sum(jnp.broadcast_to(energy, (heads, dk)), axis=0, keepdims=True)
-    sq[row] = jnp.broadcast_to(energy, (8, dk))
-
-    def sq_copy(o, slot_at):
+    def tail_all():
+        others = msg.at[pl.ds(0, total - 1)]
         return pltpu.make_async_remote_copy(
-            src_ref=sq.at[row],
-            dst_ref=sq.at[slot_at],
-            send_sem=q_send.at[o],
-            recv_sem=q_recv.at[slot_at],
-            device_id={"head": (row + o) % head_count},
+            src_ref=others,
+            dst_ref=others,
+            send_sem=t_send.at[0],
+            recv_sem=t_recv.at[0],
+            device_id={"seq": peer[0]},
             device_id_type=MESH,
         )
 
-    for o in range(1, head_count):
-        sq_copy(o, row).start()
-    for o in range(1, head_count):
-        sq_copy(o, (row + o) % head_count).wait_recv()
-    whole = sq[0]
-    for r in range(1, head_count):
-        whole = whole + sq[r]
-    count = heads * tok * seq_count * head_count
-    factor = jnp.minimum(1.0, lax.rsqrt(whole[0:1] / count + 1e-6))
-    gg_ref[...] = (local_tail + my_later) * factor
-
-    for o in range(1, seq_count):
-        dec_copy(o, place).wait_send()
-
-        @pl.when((place + o) % seq_count != dec_recv[0])
-        def _(o=o):
-            device = (place + o) % seq_count
-
-            @pl.when((device != dec_recv[1]) & (device != dec_recv[2]))
-            def _():
-                wait_dec(device)
-
+    pl.semaphore_wait(plane_sem, head_count - 1)
+    for o in reversed(range(head_count)):
+        for n in reversed(range(seq_count)):
+            if (o, n) != (0, 0):
+                tail_copy((row + o) % head_count, (place + n) % seq_count).start()
+
+    finish_out(own_pair + chunks - 1)
+    finish_out(far_pair + chunks - 1)
+    for l in range(levels):
+        if l > span_bits and l not in slots:
+            gl_ref[l] = jnp.zeros((heads, tok), F32)
+
+    for n in range(2):
+        dec_copy(n).wait_send()
     p_copy().wait_send()
     for c in range(chunks):
         a_copy(c).wait_send()
@@ -1008,10 +1025,27 @@
             b_copy(c).wait_send()
             xb_copy(c).wait_send()
 
-    for o in range(1, seq_count):
-        tot_copy(o, place).wait_send()
-    for o in range(1, head_count):
-        sq_copy(o, row).wait_send()
+    tail_all().wait_send()
+    tail_all().wait_recv()
+    rows = msg[:, 0, :]
+    row_u = lax.broadcasted_iota(jnp.int32, (total, total), 0)
+    row_v = lax.broadcasted_iota(jnp.int32, (total, total), 1)
+    behind = (row_u // seq_count == row_v // seq_count) & (row_v > row_u)
+    after_rows = lax.dot_general(
+        behind.astype(F32), rows, NN, precision=lax.Precision.HIGHEST, preferred_element_type=F32
+    )
+    plain = pltpu.roll(rows, dk - heads, 1)
+    square = pltpu.roll(rows, dk - 2 * heads, 1)
+    energy = square + after_rows * (2.0 * plain + tok * after_rows)
+    lane_all = lax.broadcasted_iota(jnp.int32, (total, dk), 1)
+    slot_all = lax.broadcasted_iota(jnp.int32, (total, dk), 0)
+    energy = jnp.sum(jnp.where(lane_all < heads, energy, 0.0), axis=0, keepdims=True)
+    whole = jnp.sum(energy, axis=1, keepdims=True)
+    my_row = jnp.sum(jnp.where(slot_all == slot, after_rows, 0.0), axis=0, keepdims=True)
+    my_later = jnp.sum(jnp.where(lane == head, my_row, 0.0), axis=1, keepdims=True)
+    count = heads * tok * total
+    factor = jnp.minimum(1.0, lax.rsqrt(whole / count + 1e-6))
+    gg_ref[...] = (local_tail + my_later) * factor
 
 
 def write_out(count, *refs):
@@ -1079,11 +1113,15 @@
         dma((head_count,)),
         dma((head_count,)),
     ]
+    args = (queries, keys, values, out_grad, log_gate, level_weight, doc_start.reshape(1, tok))
+    spec = pl.BlockSpec(memory_space=pltpu.VMEM)
+    in_spec = spec
     body = kernel
     chunks = half // group
-    if bits == 3 and chunks * group == half:
+    if bits == 3 and chunks * group == half and tok == dk and 3 * heads <= dk:
         body = chunked_kernel
-        scratch = scratch[:12] + [
+        inputs = [(x.shape, x.dtype) for x in args]
+        scratch = [vmem(*x) for x in inputs] + scratch[:12] + [
             vmem((3, 2, heads, dk), F32),
             vmem((1 + slots, heads) + block, F32),
             vmem((half,) + block, F32),
@@ -1092,9 +1130,9 @@
             vmem((half,) + block, F32),
             vmem((half,) + block, F32),
             vmem((bits + 1, heads) + block, F32),
-            vmem((seq_count, 1, dk), F32),
-            vmem((seq_count, heads, tok), F32),
-            vmem((head_count, 8, dk), F32),
+            vmem((4, 1, dk), F32),
+            vmem((seq_count * head_count, 1, dk), F32),
+            dma((7,)),
             dma((chunks,)),
             dma((chunks,)),
             dma((chunks,)),
@@ -1109,14 +1147,14 @@
             dma((chunks,)),
             dma((2, chunks)),
             dma((2, chunks)),
-            dma((seq_count,)),
-            dma((seq_count,)),
-            dma((seq_count,)),
-            dma((seq_count,)),
-            dma((head_count,)),
-            dma((head_count,)),
+            dma((2,)),
+            dma((2,)),
+            dma((1,)),
+            dma((1,)),
+            pltpu.SemaphoreType.REGULAR((max(1, head_count - 2),)),
+            pltpu.SemaphoreType.REGULAR,
         ]
-    spec = pl.BlockSpec(memory_space=pltpu.VMEM)
+        in_spec = pl.BlockSpec(memory_space=pltpu.HBM)
     outs = [
         (queries.shape, BF16),
         (keys.shape, BF16),
@@ -1127,11 +1165,11 @@
     results = pl.pallas_call(
         functools.partial(body, seq_count, head_count),
         out_shape=tuple(vmem(shape, dtype) for shape, dtype in outs),
-        in_specs=[spec] * 7,
+        in_specs=[in_spec] * 7,
         out_specs=(spec,) * 5,
         scratch_shapes=scratch,
         compiler_params=pltpu.CompilerParams(collective_id=0, has_side_effects=True),
-    )(queries, keys, values, out_grad, log_gate, level_weight, doc_start.reshape(1, tok))
+    )(*args)
     count = len(outs)
     return pl.pallas_call(
         functools.partial(write_out, count),

time: 33.8 us -> 33.8 us (level)
  no operation moved by 1% of the time
where the time goes in v3:
time: 33.8 us; the launch traced here: 33.5 us
  Pallas kernels  32.9 us (97%)
  between operations  0.64 us (2%)
    pallas_call x1, Pallas kernels, shards(): pl.pallas_call(functools.partial(body, seq_count, head_count), out_shape=...  31.8 us
    pallas_call x1, Pallas kernels, shards(): pl.pallas_call(functools.partial(write_out, count), out_shape=tuple((jax....  1.1 us

profile of v3, /device:TPU:0, one launch (start us, length us, event | category | flops | bytes accessed | tf_op | source)
XLA Modules:
  0.0 33.5 jit_solution(14603283095027560466)
XLA Ops:
  0.6 31.8 %shard_map.110 = (bf16[128,2048]{1,0:T(8,128)(2,1)S(1)}, bf16[128,2048]{1,0:T(8,128)(2,1)S(1)}, bf16[128,1024]{1,0:T(8,128)(2,1)S(1)}, f32[6,16,128]{2,1,0:T(8,128)S(1)}, f32[16,128]{1,0:T(8,128)S(1)}) custom-call(bf16[128,2048]{1,0:T(8,128)(2,1)} %q_hbm.1, bf16[128,2048]{1,0:T(8,128)(2,1)} %k_hbm.1, bf16[128,1024]{1,0:T(8,128)(2,1)} %v_hbm.1, ...), custom_call_target="tpu_custom_call" | custom-call | tf_op jit(solution)/shard_map/pallas_call | solution.py:1165
  32.4 1.1 %shard_map.111 = (bf16[128,2048]{1,0:T(8,128)(2,1)}, bf16[128,2048]{1,0:T(8,128)(2,1)}, bf16[128,1024]{1,0:T(8,128)(2,1)}, f32[6,16,128]{2,1,0:T(8,128)}, f32[16,128]{1,0:T(8,128)}) custom-call(bf16[128,2048]{1,0:T(8,128)(2,1)S(1)} %get-tuple-element.10.refs_0_, bf16[128,2048]{1,0:T(8,128)(2,1)S(1)} %get-tuple-element.11.refs_1_, ...), custom_call_target="tpu_custom_call" | custom-call | tf_op jit(solution)/shard_map/pallas_call | solution.py:1174

commit v4 on v3

--- a/solution.py
+++ b/solution.py
@@ -725,8 +725,11 @@
             st.at[kind_b, of(theirs, c)], got_b.at[at(c)], b_send.at[c], b_recv.at[c], 0
         )
 
-    def p_copy():
-        return remote(st.at[core * kind[0]], lvl.at[0], p_send.at[0], p_recv.at[0], 0)
+    def p_copy(n):
+        part = pl.ds(n * half, half)
+        return remote(
+            st.at[core * kind[0], part], lvl.at[0, part], p_send.at[n], p_recv.at[n], 0
+        )
 
     def xa_copy(c):
         return remote(
@@ -746,13 +749,6 @@
     dec_copy(0).start()
     for c in range(chunks):
         a_copy(c).start()
-
-    @pl.when(first_chip == 0)
-    def _():
-        for c in range(chunks):
-            b_copy(c).start()
-
-    p_copy().start()
 
     span_of = lax.broadcasted_iota(jnp.int32, (1, tok), 1) // SPAN
 
@@ -818,8 +814,28 @@
             cb = mix_s[n, 1, pl.ds(mine + r, 1), :]
             put[r] = ca * own_at(r) + cb * got_at(r)
 
-    lax.fori_loop(0, 2, local, 0, unroll=2)
-
+    def local_pairs(first, last):
+        lax.fori_loop(first, last, local, 0, unroll=2)
+
+    def x_start(n):
+        if n < chunks:
+            xa_copy(n).start()
+        else:
+
+            @pl.when(first_chip == 0)
+            def _():
+                xb_copy(n - chunks).start()
+
+    def x_sent(n):
+        if n < chunks:
+            xa_copy(n).wait_send()
+        else:
+
+            @pl.when(first_chip == 0)
+            def _():
+                xb_copy(n - chunks).wait_send()
+
+    local_pairs(0, 2)
     dec_copy(0).wait_recv()
     decs[2] = decs[0] * decs[1]
     d_self, d_pair = spread([decs[0], decs[1]])
@@ -828,23 +844,32 @@
     for c in range(chunks):
         a_copy(c).wait_recv()
         combine(0, c, lambda r: st[kind_a, mine + r], lambda r: got_a[r], sum_a)
-        xa_copy(c).start()
-
-    dec_copy(1).start()
+        if c < 2:
+            x_start(c)
+        if c == 1:
+            dec_copy(1).start()
+
+            @pl.when(first_chip == 0)
+            def _():
+                for n in range(chunks):
+                    b_copy(n).start()
+
+    local_pairs(2, 4)
 
     @pl.when(first_chip == 0)
     def _():
         for c in range(chunks):
             b_copy(c).wait_recv()
             combine(1, c, lambda r: st[kind_b, mine + r], lambda r: got_b[r], sum_b)
-            xb_copy(c).start()
-
-    lax.fori_loop(2, pairs - 2, local, 0, unroll=2)
 
     for r in range(1, rounds + 1):
         pl.semaphore_wait(round_sem.at[r - 1], has_next + has_last)
         if r < rounds:
             greet(round_sem.at[r])
+    x_sent(0)
+    x_start(2)
+    p_copy(0).start()
+    local_pairs(4, 6)
     dec_copy(1).wait_recv()
     (d_side,) = spread([decs[3]])
     weigh(2, x + y, d_side, d_self * d_pair)
@@ -857,7 +882,9 @@
         if got is not None:
             inner_f = inner_f * (up * got + (1.0 - up))
             inner_b = inner_b * ((1.0 - up) * got + up)
-
+    x_sent(1)
+    x_start(3)
+    p_copy(1).start()
     for c in range(chunks):
         xa_copy(c).wait_recv()
         combine(2, c, lambda r: sum_a[r], lambda r: lvl[slot_in, mine + r], sum_q)
@@ -867,8 +894,10 @@
         def _(c=c):
             f_copy(1, mine, c).start()
 
+        x_sent(c + 2)
+        x_start(c + 4)
         if c == 0:
-            lax.fori_loop(pairs - 2, pairs, local, 0, unroll=2)
+            local_pairs(6, pairs)
 
     def incoming(h):
         blocks = [lvl[b, h] for b in range(bits)]
@@ -931,16 +960,17 @@
 
     own_pair = core * chunks
     far_pair = (1 - core) * chunks
-    p_copy().wait_recv()
+    for n in range(2):
+        p_copy(n).wait_recv()
     for c in range(chunks):
+        y_copy(c).wait_recv()
+        f_copy(2, mine, c).start()
 
         @pl.when(second_chip == 0)
         def _(c=c):
             xb_copy(c).wait_recv()
             f_copy(1, mine, c).start()
 
-        y_copy(c).wait_recv()
-        f_copy(2, mine, c).start()
         if c == 0:
             for o in range(1, head_count):
                 pl.semaphore_signal(
@@ -950,13 +980,9 @@
                     device_id_type=MESH,
                 )
         finish_drift(own_pair + c)
-        if c < chunks - 1:
-            finish_out(own_pair + c)
         for j in (1, 2):
             f_copy(j, theirs, c).wait_recv()
         finish_drift(far_pair + c)
-        if c < chunks - 1:
-            finish_out(far_pair + c)
 
     later = (rows_i >= cols_i).astype(F32)
     local_tail = lax.dot_general(
@@ -1003,18 +1029,23 @@
             if (o, n) != (0, 0):
                 tail_copy((row + o) % head_count, (place + n) % seq_count).start()
 
-    finish_out(own_pair + chunks - 1)
-    finish_out(far_pair + chunks - 1)
+    def outputs(p, _):
+        finish_out(p)
+        return 0
+
+    lax.fori_loop(0, pairs, outputs, 0, unroll=2)
     for l in range(levels):
         if l > span_bits and l not in slots:
             gl_ref[l] = jnp.zeros((heads, tok), F32)
 
     for n in range(2):
         dec_copy(n).wait_send()
-    p_copy().wait_send()
+    for n in range(2):
+        p_copy(n).wait_send()
+    for n in range(chunks + 2, 2 * chunks):
+        x_sent(n)
     for c in range(chunks):
         a_copy(c).wait_send()
-        xa_copy(c).wait_send()
         y_copy(c).wait_send()
         for j in (1, 2):
             f_copy(j, mine, c).wait_send()
@@ -1023,7 +1054,6 @@
     def _():
         for c in range(chunks):
             b_copy(c).wait_send()
-            xb_copy(c).wait_send()
 
     tail_all().wait_send()
     tail_all().wait_recv()
@@ -1118,7 +1148,7 @@
     in_spec = spec
     body = kernel
     chunks = half // group
-    if bits == 3 and chunks * group == half and tok == dk and 3 * heads <= dk:
+    if bits == 3 and chunks == 4 and chunks * group == half and tok == dk and 3 * heads <= dk:
         body = chunked_kernel
         inputs = [(x.shape, x.dtype) for x in args]
         scratch = [vmem(*x) for x in inputs] + scratch[:12] + [
@@ -1137,8 +1167,8 @@
             dma((chunks,)),
             dma((chunks,)),
             dma((chunks,)),
-            dma((1,)),
-            dma((1,)),
+            dma((2,)),
+            dma((2,)),
             dma((chunks,)),
             dma((chunks,)),
             dma((chunks,)),

time: 33.8 us -> 32.5 us (0.962)
  Pallas kernels: 32.9 us -> 31.6 us
    pallas_call x1, Pallas kernels: 31.8 us -> 30.5 us  [shards(): pl.pallas_call(functools.partial(body, seq_count, head_count), out_shape=...]
where the time goes in v4:
time: 32.5 us; the launch traced here: 32.3 us
  Pallas kernels  31.6 us (97%)
  between operations  0.64 us (2%)
    pallas_call x1, Pallas kernels, shards(): pl.pallas_call(functools.partial(body, seq_count, head_count), out_shape=...  30.5 us
    pallas_call x1, Pallas kernels, shards(): pl.pallas_call(functools.partial(write_out, count), out_shape=tuple((jax....  1.1 us

profile of v4, /device:TPU:0, one launch (start us, length us, event | category | flops | bytes accessed | tf_op | source)
XLA Modules:
  0.0 32.3 jit_solution(3609941379977956781)
XLA Ops:
  0.6 30.5 %shard_map.110 = (bf16[128,2048]{1,0:T(8,128)(2,1)S(1)}, bf16[128,2048]{1,0:T(8,128)(2,1)S(1)}, bf16[128,1024]{1,0:T(8,128)(2,1)S(1)}, f32[6,16,128]{2,1,0:T(8,128)S(1)}, f32[16,128]{1,0:T(8,128)S(1)}) custom-call(bf16[128,2048]{1,0:T(8,128)(2,1)} %q_hbm.1, bf16[128,2048]{1,0:T(8,128)(2,1)} %k_hbm.1, bf16[128,1024]{1,0:T(8,128)(2,1)} %v_hbm.1, ...), custom_call_target="tpu_custom_call" | custom-call | tf_op jit(solution)/shard_map/pallas_call | solution.py:1195
  31.2 1.1 %shard_map.111 = (bf16[128,2048]{1,0:T(8,128)(2,1)}, bf16[128,2048]{1,0:T(8,128)(2,1)}, bf16[128,1024]{1,0:T(8,128)(2,1)}, f32[6,16,128]{2,1,0:T(8,128)}, f32[16,128]{1,0:T(8,128)}) custom-call(bf16[128,2048]{1,0:T(8,128)(2,1)S(1)} %get-tuple-element.10.refs_0_, bf16[128,2048]{1,0:T(8,128)(2,1)S(1)} %get-tuple-element.11.refs_1_, ...), custom_call_target="tpu_custom_call" | custom-call | tf_op jit(solution)/shard_map/pallas_call | solution.py:1204

commit v5 on v4

--- a/solution.py
+++ b/solution.py
@@ -685,7 +685,12 @@
 
     for n in range(2, 7):
         load(n).wait()
-    lax.fori_loop(0, pairs, states, 0, unroll=2)
+    own_pair = core * chunks
+    far_pair = (1 - core) * chunks
+    def states_from(base):
+        lax.fori_loop(0, 2, lambda n, _: states(base + n, 0), 0, unroll=2)
+
+    states_from(far_pair)
     pl.semaphore_wait(barrier, bits + has_next + has_last)
     rounds = head_count - 2
     if rounds > 0:
@@ -731,13 +736,23 @@
             st.at[core * kind[0], part], lvl.at[0, part], p_send.at[n], p_recv.at[n], 0
         )
 
-    def xa_copy(c):
+    piece = 2
+    pieces = half // piece
+
+    def xa_copy(n):
+        here = pl.ds(n * piece, piece)
+        there = pl.ds(mine + n * piece, piece)
         return remote(
-            sum_a.at[at(c)], lvl.at[slot_out, of(mine, c)], xa_send.at[c], xa_recv.at[c], 1
-        )
-
-    def xb_copy(c):
-        return remote(sum_b.at[at(c)], lvl.at[1, of(mine, c)], xb_send.at[c], xb_recv.at[c], 1)
+            sum_a.at[here], lvl.at[slot_out, there], xa_send.at[n], xa_recv.at[n], 1
+        )
+
+    def xb_copy(n):
+        here = pl.ds(n * piece, piece)
+        there = pl.ds(mine + n * piece, piece)
+        return remote(sum_b.at[here], lvl.at[1, there], xb_send.at[n], xb_recv.at[n], 1)
+
+    def pieces_of(c):
+        return range(c * group // piece, (c + 1) * group // piece)
 
     def y_copy(c):
         return remote(sum_q.at[at(c)], lvl.at[2, of(mine, c)], y_send.at[c], y_recv.at[c], 2)
@@ -747,8 +762,13 @@
         return remote(part, part, f_send.at[j - 1, c], f_recv.at[j - 1, c], 0)
 
     dec_copy(0).start()
-    for c in range(chunks):
+    for c in range(2):
         a_copy(c).start()
+    states_from(far_pair + 2)
+    for c in range(2, chunks):
+        a_copy(c).start()
+    states_from(own_pair)
+    states_from(own_pair + 2)
 
     span_of = lax.broadcasted_iota(jnp.int32, (1, tok), 1) // SPAN
 
@@ -818,24 +838,29 @@
         lax.fori_loop(first, last, local, 0, unroll=2)
 
     def x_start(n):
-        if n < chunks:
+        if n < pieces:
             xa_copy(n).start()
-        else:
+        elif n < 2 * pieces:
 
             @pl.when(first_chip == 0)
             def _():
-                xb_copy(n - chunks).start()
+                xb_copy(n - pieces).start()
 
     def x_sent(n):
-        if n < chunks:
+        if n < pieces:
             xa_copy(n).wait_send()
         else:
 
             @pl.when(first_chip == 0)
             def _():
-                xb_copy(n - chunks).wait_send()
-
-    local_pairs(0, 2)
+                xb_copy(n - pieces).wait_send()
+
+    ahead = 2
+
+    def x_next(n):
+        x_sent(n)
+        x_start(n + ahead)
+
     dec_copy(0).wait_recv()
     decs[2] = decs[0] * decs[1]
     d_self, d_pair = spread([decs[0], decs[1]])
@@ -844,8 +869,9 @@
     for c in range(chunks):
         a_copy(c).wait_recv()
         combine(0, c, lambda r: st[kind_a, mine + r], lambda r: got_a[r], sum_a)
-        if c < 2:
-            x_start(c)
+        for n in pieces_of(c):
+            if n < ahead:
+                x_start(n)
         if c == 1:
             dec_copy(1).start()
 
@@ -854,7 +880,7 @@
                 for n in range(chunks):
                     b_copy(n).start()
 
-    local_pairs(2, 4)
+    local_pairs(0, 4)
 
     @pl.when(first_chip == 0)
     def _():
@@ -866,8 +892,7 @@
         pl.semaphore_wait(round_sem.at[r - 1], has_next + has_last)
         if r < rounds:
             greet(round_sem.at[r])
-    x_sent(0)
-    x_start(2)
+    x_next(0)
     p_copy(0).start()
     local_pairs(4, 6)
     dec_copy(1).wait_recv()
@@ -882,22 +907,26 @@
         if got is not None:
             inner_f = inner_f * (up * got + (1.0 - up))
             inner_b = inner_b * ((1.0 - up) * got + up)
-    x_sent(1)
-    x_start(3)
+    x_next(1)
     p_copy(1).start()
-    for c in range(chunks):
-        xa_copy(c).wait_recv()
+    def turn(c):
+        for n in pieces_of(c):
+            xa_copy(n).wait_recv()
         combine(2, c, lambda r: sum_a[r], lambda r: lvl[slot_in, mine + r], sum_q)
         y_copy(c).start()
 
         @pl.when(second_chip == 1)
-        def _(c=c):
+        def _():
             f_copy(1, mine, c).start()
 
-        x_sent(c + 2)
-        x_start(c + 4)
-        if c == 0:
-            local_pairs(6, pairs)
+    turn(0)
+    local_pairs(6, pairs)
+    x_next(2)
+    turn(1)
+    x_next(3)
+    turn(2)
+    x_next(4)
+    turn(3)
 
     def incoming(h):
         blocks = [lvl[b, h] for b in range(bits)]
@@ -958,17 +987,18 @@
             gk_ref[:, wide] = (gk_s[h] + gk_in).astype(BF16)
         gv_ref[:, lanes] = jnp.transpose(vg_s[p]).astype(BF16)
 
-    own_pair = core * chunks
-    far_pair = (1 - core) * chunks
     for n in range(2):
         p_copy(n).wait_recv()
     for c in range(chunks):
+        for n in ((5,), (), (), ())[c]:
+            x_next(n)
         y_copy(c).wait_recv()
         f_copy(2, mine, c).start()
 
         @pl.when(second_chip == 0)
         def _(c=c):
-            xb_copy(c).wait_recv()
+            for n in pieces_of(c):
+                xb_copy(n).wait_recv()
             f_copy(1, mine, c).start()
 
         if c == 0:
@@ -1042,7 +1072,7 @@
         dec_copy(n).wait_send()
     for n in range(2):
         p_copy(n).wait_send()
-    for n in range(chunks + 2, 2 * chunks):
+    for n in range(2 * pieces - ahead, 2 * pieces):
         x_sent(n)
     for c in range(chunks):
         a_copy(c).wait_send()
@@ -1169,10 +1199,10 @@
             dma((chunks,)),
             dma((2,)),
             dma((2,)),
-            dma((chunks,)),
-            dma((chunks,)),
-            dma((chunks,)),
-            dma((chunks,)),
+            dma((half,)),
+            dma((half,)),
+            dma((half,)),
+            dma((half,)),
             dma((chunks,)),
             dma((chunks,)),
             dma((2, chunks)),

time: 32.5 us -> 31.3 us (0.963)
  Pallas kernels: 31.6 us -> 30.5 us
    pallas_call x1, Pallas kernels: 30.5 us -> 29.4 us  [shards(): pl.pallas_call(functools.partial(body, seq_count, head_count), out_shape=...]
where the time goes in v5:
time: 31.3 us; the launch traced here: 31.1 us
  Pallas kernels  30.5 us (97%)
  between operations  0.64 us (2%)
    pallas_call x1, Pallas kernels, shards(): pl.pallas_call(functools.partial(body, seq_count, head_count), out_shape=...  29.4 us
    pallas_call x1, Pallas kernels, shards(): pl.pallas_call(functools.partial(write_out, count), out_shape=tuple((jax....  1.1 us

profile of v5, /device:TPU:0, one launch (start us, length us, event | category | flops | bytes accessed | tf_op | source)
XLA Modules:
  0.0 31.1 jit_solution(9828484033649731382)
XLA Ops:
  0.6 29.4 %shard_map.110 = (bf16[128,2048]{1,0:T(8,128)(2,1)S(1)}, bf16[128,2048]{1,0:T(8,128)(2,1)S(1)}, bf16[128,1024]{1,0:T(8,128)(2,1)S(1)}, f32[6,16,128]{2,1,0:T(8,128)S(1)}, f32[16,128]{1,0:T(8,128)S(1)}) custom-call(bf16[128,2048]{1,0:T(8,128)(2,1)} %q_hbm.1, bf16[128,2048]{1,0:T(8,128)(2,1)} %k_hbm.1, bf16[128,1024]{1,0:T(8,128)(2,1)} %v_hbm.1, ...), custom_call_target="tpu_custom_call" | custom-call | tf_op jit(solution)/shard_map/pallas_call | solution.py:1225
  30.0 1.1 %shard_map.111 = (bf16[128,2048]{1,0:T(8,128)(2,1)}, bf16[128,2048]{1,0:T(8,128)(2,1)}, bf16[128,1024]{1,0:T(8,128)(2,1)}, f32[6,16,128]{2,1,0:T(8,128)}, f32[16,128]{1,0:T(8,128)}) custom-call(bf16[128,2048]{1,0:T(8,128)(2,1)S(1)} %get-tuple-element.10.refs_0_, bf16[128,2048]{1,0:T(8,128)(2,1)S(1)} %get-tuple-element.11.refs_1_, ...), custom_call_target="tpu_custom_call" | custom-call | tf_op jit(solution)/shard_map/pallas_call | solution.py:1234

commit v6 on v5

--- a/solution.py
+++ b/solution.py
@@ -23,6 +23,19 @@
 def split(x):
     high = x.astype(BF16)
     return high, (x - high.astype(F32)).astype(BF16)
+
+
+def pieces_exact(x):
+    high = x.astype(BF16)
+    rest = x - high.astype(F32)
+    middle = rest.astype(BF16)
+    return high, middle, (rest - middle.astype(F32)).astype(BF16)
+
+
+def dot_exact(x, b):
+    rows = x.shape[0]
+    out = dot(jnp.concatenate(pieces_exact(x), axis=0), b, NN)
+    return out[:rows] + out[rows : 2 * rows] + out[2 * rows :]
 
 
 def dot_fine(x, b, dims):
@@ -533,7 +546,8 @@
     gk_ref,
     gv_ref,
     gl_ref,
-    gg_ref,
+    tail_ref,
+    msg,
     q_ref,
     k_ref,
     v_ref,
@@ -562,7 +576,6 @@
     sum_q,
     lvl,
     decs,
-    msg,
     i_sem,
     a_send,
     a_recv,
@@ -638,12 +651,10 @@
 
     rows_i = lax.broadcasted_iota(jnp.int32, (tok, tok), 0)
     cols_i = lax.broadcasted_iota(jnp.int32, (tok, tok), 1)
-    tri = (rows_i <= cols_i).astype(F32)
+    tri = (rows_i <= cols_i).astype(BF16)
     starts = jnp.broadcast_to(ds_ref[...].astype(F32), (8, tok))
     both = jnp.concatenate([lg_ref[...], starts], axis=0)
-    cum_all = lax.dot_general(
-        both, tri, NN, precision=lax.Precision.HIGHEST, preferred_element_type=F32
-    )
+    cum_all = dot_exact(both, tri)
     cum_t = jnp.transpose(
         jnp.concatenate([cum_all, jnp.zeros((dk - heads - 8, tok), F32)], axis=0)
     )
@@ -736,7 +747,7 @@
             st.at[core * kind[0], part], lvl.at[0, part], p_send.at[n], p_recv.at[n], 0
         )
 
-    piece = 2
+    piece = 1
     pieces = half // piece
 
     def xa_copy(n):
@@ -754,8 +765,10 @@
     def pieces_of(c):
         return range(c * group // piece, (c + 1) * group // piece)
 
-    def y_copy(c):
-        return remote(sum_q.at[at(c)], lvl.at[2, of(mine, c)], y_send.at[c], y_recv.at[c], 2)
+    def y_copy(n):
+        here = pl.ds(n * piece, piece)
+        there = pl.ds(mine + n * piece, piece)
+        return remote(sum_q.at[here], lvl.at[2, there], y_send.at[n], y_recv.at[n], 2)
 
     def f_copy(j, base, c):
         part = lvl.at[j, of(base, c)]
@@ -855,7 +868,7 @@
             def _():
                 xb_copy(n - pieces).wait_send()
 
-    ahead = 2
+    ahead = 5
 
     def x_next(n):
         x_sent(n)
@@ -893,6 +906,7 @@
         if r < rounds:
             greet(round_sem.at[r])
     x_next(0)
+    x_next(1)
     p_copy(0).start()
     local_pairs(4, 6)
     dec_copy(1).wait_recv()
@@ -907,26 +921,38 @@
         if got is not None:
             inner_f = inner_f * (up * got + (1.0 - up))
             inner_b = inner_b * ((1.0 - up) * got + up)
-    x_next(1)
+    x_next(2)
+    x_next(3)
     p_copy(1).start()
-    def turn(c):
-        for n in pieces_of(c):
-            xa_copy(n).wait_recv()
-        combine(2, c, lambda r: sum_a[r], lambda r: lvl[slot_in, mine + r], sum_q)
-        y_copy(c).start()
-
-        @pl.when(second_chip == 1)
-        def _():
-            f_copy(1, mine, c).start()
+    def turn(n):
+        xa_copy(n).wait_recv()
+        for r in range(n * piece, (n + 1) * piece):
+            ca = mix_s[2, 0, pl.ds(mine + r, 1), :]
+            cb = mix_s[2, 1, pl.ds(mine + r, 1), :]
+            sum_q[r] = ca * sum_a[r] + cb * lvl[slot_in, mine + r]
+        y_copy(n).start()
+        if (n + 1) * piece % group == 0:
+
+            @pl.when(second_chip == 1)
+            def _():
+                f_copy(1, mine, n * piece // group).start()
 
     turn(0)
     local_pairs(6, pairs)
-    x_next(2)
+    x_next(4)
     turn(1)
-    x_next(3)
+    x_next(5)
     turn(2)
-    x_next(4)
+    x_next(6)
     turn(3)
+    x_next(7)
+    turn(4)
+    x_next(8)
+    turn(5)
+    turn(6)
+    x_next(9)
+    x_next(10)
+    turn(7)
 
     def incoming(h):
         blocks = [lvl[b, h] for b in range(bits)]
@@ -990,9 +1016,10 @@
     for n in range(2):
         p_copy(n).wait_recv()
     for c in range(chunks):
-        for n in ((5,), (), (), ())[c]:
+        for n in ((), (), (), ())[c]:
             x_next(n)
-        y_copy(c).wait_recv()
+        for n in pieces_of(c):
+            y_copy(n).wait_recv()
         f_copy(2, mine, c).start()
 
         @pl.when(second_chip == 0)
@@ -1014,10 +1041,9 @@
             f_copy(j, theirs, c).wait_recv()
         finish_drift(far_pair + c)
 
-    later = (rows_i >= cols_i).astype(F32)
-    local_tail = lax.dot_general(
-        drift_s[...], later, NN, precision=lax.Precision.HIGHEST, preferred_element_type=F32
-    )
+    later = (rows_i >= cols_i).astype(BF16)
+    local_tail = dot_exact(drift_s[...], later)
+    tail_ref[...] = local_tail
     lane = lax.broadcasted_iota(jnp.int32, (heads, tok), 1)
     head = lax.broadcasted_iota(jnp.int32, (heads, tok), 0)
     sums = [
@@ -1054,8 +1080,8 @@
         )
 
     pl.semaphore_wait(plane_sem, head_count - 1)
-    for o in reversed(range(head_count)):
-        for n in reversed(range(seq_count)):
+    for o in list(range(1, head_count)) + [0]:
+        for n in list(range(1, seq_count)) + [0]:
             if (o, n) != (0, 0):
                 tail_copy((row + o) % head_count, (place + n) % seq_count).start()
 
@@ -1076,7 +1102,8 @@
         x_sent(n)
     for c in range(chunks):
         a_copy(c).wait_send()
-        y_copy(c).wait_send()
+        for n in pieces_of(c):
+            y_copy(n).wait_send()
         for j in (1, 2):
             f_copy(j, mine, c).wait_send()
 
@@ -1087,13 +1114,48 @@
 
     tail_all().wait_send()
     tail_all().wait_recv()
+
+
+def finish_kernel(
+    seq_count,
+    head_count,
+    gq_ref,
+    gk_ref,
+    gv_ref,
+    gl_ref,
+    tail_ref,
+    msg,
+    gq_out,
+    gk_out,
+    gv_out,
+    gl_out,
+    gg_out,
+    gg_s,
+    sems,
+):
+    copies = [
+        pltpu.make_async_copy(src, dst, sems.at[n])
+        for n, (src, dst) in enumerate(
+            (
+                (gq_ref, gq_out),
+                (gk_ref, gk_out),
+                (gv_ref, gv_out),
+                (gl_ref, gl_out),
+                (gg_s, gg_out),
+            )
+        )
+    ]
+    for c in copies[:4]:
+        c.start()
+    heads, tok = tail_ref.shape
+    dk = msg.shape[2]
+    total = seq_count * head_count
+    slot = lax.axis_index("head") * seq_count + lax.axis_index("seq")
     rows = msg[:, 0, :]
     row_u = lax.broadcasted_iota(jnp.int32, (total, total), 0)
     row_v = lax.broadcasted_iota(jnp.int32, (total, total), 1)
-    behind = (row_u // seq_count == row_v // seq_count) & (row_v > row_u)
-    after_rows = lax.dot_general(
-        behind.astype(F32), rows, NN, precision=lax.Precision.HIGHEST, preferred_element_type=F32
-    )
+    behind = ((row_u // seq_count == row_v // seq_count) & (row_v > row_u)).astype(BF16)
+    after_rows = sum(dot(behind, piece, NN) for piece in pieces_exact(rows))
     plain = pltpu.roll(rows, dk - heads, 1)
     square = pltpu.roll(rows, dk - 2 * heads, 1)
     energy = square + after_rows * (2.0 * plain + tok * after_rows)
@@ -1102,10 +1164,15 @@
     energy = jnp.sum(jnp.where(lane_all < heads, energy, 0.0), axis=0, keepdims=True)
     whole = jnp.sum(energy, axis=1, keepdims=True)
     my_row = jnp.sum(jnp.where(slot_all == slot, after_rows, 0.0), axis=0, keepdims=True)
+    lane = lax.broadcasted_iota(jnp.int32, (heads, dk), 1)
+    head = lax.broadcasted_iota(jnp.int32, (heads, dk), 0)
     my_later = jnp.sum(jnp.where(lane == head, my_row, 0.0), axis=1, keepdims=True)
     count = heads * tok * total
     factor = jnp.minimum(1.0, lax.rsqrt(whole / count + 1e-6))
-    gg_ref[...] = (local_tail + my_later) * factor
+    gg_s[...] = (tail_ref[...] + my_later) * factor
+    copies[4].start()
+    for c in copies:
+        c.wait()
 
 
 def write_out(count, *refs):
@@ -1191,7 +1258,6 @@
             vmem((half,) + block, F32),
             vmem((bits + 1, heads) + block, F32),
             vmem((4, 1, dk), F32),
-            vmem((seq_count * head_count, 1, dk), F32),
             dma((7,)),
             dma((chunks,)),
             dma((chunks,)),
@@ -1203,8 +1269,8 @@
             dma((half,)),
             dma((half,)),
             dma((half,)),
-            dma((chunks,)),
-            dma((chunks,)),
+            dma((half,)),
+            dma((half,)),
             dma((2, chunks)),
             dma((2, chunks)),
             dma((2,)),
@@ -1222,21 +1288,28 @@
         (level_weight.shape, F32),
         (log_gate.shape, F32),
     ]
+    held = list(outs)
+    writer = (write_out, len(outs))
+    writer_scratch = []
+    if body is chunked_kernel:
+        held.append(((seq_count * head_count, 1, dk), F32))
+        writer = (finish_kernel, seq_count, head_count)
+        writer_scratch = [vmem(*outs[-1])]
     results = pl.pallas_call(
         functools.partial(body, seq_count, head_count),
-        out_shape=tuple(vmem(shape, dtype) for shape, dtype in outs),
+        out_shape=tuple(vmem(shape, dtype) for shape, dtype in held),
         in_specs=[in_spec] * 7,
-        out_specs=(spec,) * 5,
+        out_specs=(spec,) * len(held),
         scratch_shapes=scratch,
         compiler_params=pltpu.CompilerParams(collective_id=0, has_side_effects=True),
     )(*args)
     count = len(outs)
     return pl.pallas_call(
-        functools.partial(write_out, count),
+        functools.partial(*writer),
         out_shape=tuple(jax.ShapeDtypeStruct(shape, dtype) for shape, dtype in outs),
-        in_specs=[spec] * count,
+        in_specs=[spec] * len(held),
         out_specs=(pl.BlockSpec(memory_space=pltpu.HBM),) * count,
-        scratch_shapes=[dma((count,))],
+        scratch_shapes=writer_scratch + [dma((count,))],
     )(*[pltpu.with_memory_space_constraint(r, pltpu.VMEM) for r in results])
 
 

time: 31.3 us -> 30.5 us (0.974)
  Pallas kernels: 30.5 us -> 29.6 us
    pallas_call x1, Pallas kernels: 29.4 us -> 28.5 us  [shards(): pl.pallas_call(functools.partial(body, seq_count, head_count), out_shape=...]
where the time goes in v6:
time: 30.5 us; the launch traced here: 30.2 us
  Pallas kernels  29.6 us (97%)
  between operations  0.64 us (2%)
    pallas_call x1, Pallas kernels, shards(): pl.pallas_call(functools.partial(body, seq_count, head_count), out_shape=...  28.5 us
    pallas_call x1, Pallas kernels, shards(): pl.pallas_call(functools.partial(*writer), out_shape=tuple((jax.ShapeDtyp...  1.11 us

profile of v6, /device:TPU:0, one launch (start us, length us, event | category | flops | bytes accessed | tf_op | source)
XLA Modules:
  0.0 30.2 jit_solution(1050281295915455207)
XLA Ops:
  0.6 28.5 %shard_map.110 = (bf16[128,2048]{1,0:T(8,128)(2,1)S(1)}, bf16[128,2048]{1,0:T(8,128)(2,1)S(1)}, bf16[128,1024]{1,0:T(8,128)(2,1)S(1)}, f32[6,16,128]{2,1,0:T(8,1...) custom-call(bf16[128,2048]{1,0:T(8,128)(2,1)} %q_hbm.1, bf16[128,2048]{1,0:T(8,128)(2,1)} %k_hbm.1, ...), custom_call_target="tpu_custom_call" | custom-call | tf_op jit(solution)/shard_map/pallas_call | solution.py:1298
  29.1 1.1 %shard_map.111 = (bf16[128,2048]{1,0:T(8,128)(2,1)}, bf16[128,2048]{1,0:T(8,128)(2,1)}, bf16[128,1024]{1,0:T(8,128)(2,1)}, f32[6,16,128]{2,1,0:T(8,128)}, f32[16,128]{1,0:T(8,128)}) custom-call(bf16[128,2048]{1,0:T(8,128)(2,1)S(1)} %get-tuple-element.11.gq_ref, bf16[128,2048]{1,0:T(8,128)(2,1)S(1)} %get-tuple-element.12.gk_ref, ...), custom_call_target="tpu_custom_call" | custom-call | tf_op jit(solution)/shard_map/pallas_call | solution.py:1307

commit v7 on v6

--- a/solution.py
+++ b/solution.py
@@ -575,6 +575,7 @@
     sum_b,
     sum_q,
     lvl,
+    relay,
     decs,
     i_sem,
     a_send,
@@ -591,6 +592,8 @@
     y_recv,
     f_send,
     f_recv,
+    r_send,
+    r_recv,
     d_send,
     d_recv,
     t_send,
@@ -729,7 +732,8 @@
     slot_in = bits - (bits - 1) * second_chip
 
     def dec_copy(n):
-        return remote(decs.at[2 * n], decs.at[2 * n + 1], d_send.at[n], d_recv.at[n], n)
+        src = 3 if n == 2 else 2 * n
+        return remote(decs.at[src], decs.at[2 * n + 1], d_send.at[n], d_recv.at[n], n)
 
     def a_copy(c):
         return remote(
@@ -769,6 +773,23 @@
         here = pl.ds(n * piece, piece)
         there = pl.ds(mine + n * piece, piece)
         return remote(sum_q.at[here], lvl.at[2, there], y_send.at[n], y_recv.at[n], 2)
+
+    late = range(pieces - group // piece, pieces)
+
+    def early_copy(n):
+        return remote(
+            sum_a.at[pl.ds(n * piece, piece)],
+            relay.at[0, pl.ds((n - late[0]) * piece, piece)],
+            y_send.at[n],
+            y_recv.at[n],
+            2,
+        )
+
+    def relay_copy(n):
+        part = pl.ds((n - late[0]) * piece, piece)
+        return remote(
+            relay.at[0, part], relay.at[1, part], r_send.at[n - late[0]], r_recv.at[n - late[0]], 1
+        )
 
     def f_copy(j, base, c):
         part = lvl.at[j, of(base, c)]
@@ -851,8 +872,20 @@
         lax.fori_loop(first, last, local, 0, unroll=2)
 
     def x_start(n):
-        if n < pieces:
+        if n in late:
+
+            @pl.when(y == 0)
+            def _():
+                xa_copy(n).start()
+
+        elif n < pieces:
             xa_copy(n).start()
+        elif n - pieces in late:
+
+            @pl.when((y == 1) & (first_chip == 0))
+            def _():
+                xb_copy(n - pieces).start()
+
         elif n < 2 * pieces:
 
             @pl.when(first_chip == 0)
@@ -860,7 +893,13 @@
                 xb_copy(n - pieces).start()
 
     def x_sent(n):
-        if n < pieces:
+        if n in late:
+
+            @pl.when(y == 0)
+            def _():
+                xa_copy(n).wait_send()
+
+        elif n < pieces:
             xa_copy(n).wait_send()
         else:
 
@@ -883,7 +922,7 @@
         a_copy(c).wait_recv()
         combine(0, c, lambda r: st[kind_a, mine + r], lambda r: got_a[r], sum_a)
         for n in pieces_of(c):
-            if n < ahead:
+            if n < 3:
                 x_start(n)
         if c == 1:
             dec_copy(1).start()
@@ -893,6 +932,13 @@
                 for n in range(chunks):
                     b_copy(n).start()
 
+    @pl.when(y == 1)
+    def _():
+        for n in late:
+            early_copy(n).start()
+
+    for n in range(3, ahead):
+        x_start(n)
     local_pairs(0, 4)
 
     @pl.when(first_chip == 0)
@@ -911,6 +957,7 @@
     local_pairs(4, 6)
     dec_copy(1).wait_recv()
     (d_side,) = spread([decs[3]])
+    dec_copy(2).start()
     weigh(2, x + y, d_side, d_self * d_pair)
     inner_f = jnp.ones((heads, dk), F32)
     inner_b = jnp.ones((heads, dk), F32)
@@ -925,6 +972,16 @@
     x_next(3)
     p_copy(1).start()
     def turn(n):
+        if n in late:
+
+            @pl.when(y == 0)
+            def _():
+                take_turn(n)
+
+        else:
+            take_turn(n)
+
+    def take_turn(n):
         xa_copy(n).wait_recv()
         for r in range(n * piece, (n + 1) * piece):
             ca = mix_s[2, 0, pl.ds(mine + r, 1), :]
@@ -947,6 +1004,15 @@
     turn(3)
     x_next(7)
     turn(4)
+
+    @pl.when(first_chip == 1)
+    def _():
+        for n in late:
+            early_copy(n).wait_recv()
+            relay_copy(n).start()
+            for r in range(n * piece, (n + 1) * piece):
+                lvl[2, mine + r] = jnp.zeros((dv, dk), F32)
+
     x_next(8)
     turn(5)
     turn(6)
@@ -1013,14 +1079,44 @@
             gk_ref[:, wide] = (gk_s[h] + gk_in).astype(BF16)
         gv_ref[:, lanes] = jnp.transpose(vg_s[p]).astype(BF16)
 
+    dec_copy(2).wait_recv()
+    (d_cross,) = spread([decs[5]])
+    mix_s[3, 0] = d_cross
+    mix_s[3, 1] = d_self * d_pair
+
+    def join_late():
+        @pl.when(second_chip == 1)
+        def _():
+            for n in late:
+                early_copy(n).wait_recv()
+                relay_copy(n).wait_recv()
+                for r in range(n * piece, (n + 1) * piece):
+                    ca = mix_s[3, 0, pl.ds(mine + r, 1), :]
+                    cb = mix_s[3, 1, pl.ds(mine + r, 1), :]
+                    m = r - late[0] * piece
+                    joined = ca * relay[0, m] + relay[1, m]
+                    lvl[2, mine + r] = joined
+                    sum_b[r] = sum_b[r] + cb * joined
+                xb_copy(n).start()
+
     for n in range(2):
         p_copy(n).wait_recv()
     for c in range(chunks):
         for n in ((), (), (), ())[c]:
             x_next(n)
-        for n in pieces_of(c):
-            y_copy(n).wait_recv()
+        if c == chunks - 1:
+
+            @pl.when(y == 1)
+            def _(c=c):
+                for n in pieces_of(c):
+                    y_copy(n).wait_recv()
+
+        else:
+            for n in pieces_of(c):
+                y_copy(n).wait_recv()
         f_copy(2, mine, c).start()
+        if c == 1:
+            join_late()
 
         @pl.when(second_chip == 0)
         def _(c=c):
@@ -1094,8 +1190,14 @@
         if l > span_bits and l not in slots:
             gl_ref[l] = jnp.zeros((heads, tok), F32)
 
-    for n in range(2):
+    for n in range(3):
         dec_copy(n).wait_send()
+
+    @pl.when(first_chip == 1)
+    def _():
+        for n in late:
+            relay_copy(n).wait_send()
+
     for n in range(2):
         p_copy(n).wait_send()
     for n in range(2 * pieces - ahead, 2 * pieces):
@@ -1249,7 +1351,7 @@
         body = chunked_kernel
         inputs = [(x.shape, x.dtype) for x in args]
         scratch = [vmem(*x) for x in inputs] + scratch[:12] + [
-            vmem((3, 2, heads, dk), F32),
+            vmem((4, 2, heads, dk), F32),
             vmem((1 + slots, heads) + block, F32),
             vmem((half,) + block, F32),
             vmem((half,) + block, F32),
@@ -1257,7 +1359,8 @@
             vmem((half,) + block, F32),
             vmem((half,) + block, F32),
             vmem((bits + 1, heads) + block, F32),
-            vmem((4, 1, dk), F32),
+            vmem((2, group) + block, F32),
+            vmem((6, 1, dk), F32),
             dma((7,)),
             dma((chunks,)),
             dma((chunks,)),
@@ -1273,8 +1376,10 @@
             dma((half,)),
             dma((2, chunks)),
             dma((2, chunks)),
-            dma((2,)),
-            dma((2,)),
+            dma((group,)),
+            dma((group,)),
+            dma((3,)),
+            dma((3,)),
             dma((1,)),
             dma((1,)),
             pltpu.SemaphoreType.REGULAR((max(1, head_count - 2),)),

time: 30.5 us -> 29.4 us (0.964)
  Pallas kernels: 29.6 us -> 28.5 us
    pallas_call x1, Pallas kernels: 28.5 us -> 27.4 us  [shards(): pl.pallas_call(functools.partial(body, seq_count, head_count), out_shape=...]
where the time goes in v7:
time: 29.4 us; the launch traced here: 29.1 us
  Pallas kernels  28.5 us (97%)
  between operations  0.64 us (2%)
    pallas_call x1, Pallas kernels, shards(): pl.pallas_call(functools.partial(body, seq_count, head_count), out_shape=...  27.4 us
    pallas_call x1, Pallas kernels, shards(): pl.pallas_call(functools.partial(*writer), out_shape=tuple((jax.ShapeDtyp...  1.11 us

profile of v7, /device:TPU:0, one launch (start us, length us, event | category | flops | bytes accessed | tf_op | source)
XLA Modules:
  0.0 29.1 jit_solution(15920210332814407759)
XLA Ops:
  0.6 27.4 %shard_map.110 = (bf16[128,2048]{1,0:T(8,128)(2,1)S(1)}, bf16[128,2048]{1,0:T(8,128)(2,1)S(1)}, bf16[128,1024]{1,0:T(8,128)(2,1)S(1)}, f32[6,16,128]{2,1,0:T(8,1...) custom-call(bf16[128,2048]{1,0:T(8,128)(2,1)} %q_hbm.1, bf16[128,2048]{1,0:T(8,128)(2,1)} %k_hbm.1, ...), custom_call_target="tpu_custom_call" | custom-call | tf_op jit(solution)/shard_map/pallas_call | solution.py:1403
  28.0 1.1 %shard_map.111 = (bf16[128,2048]{1,0:T(8,128)(2,1)}, bf16[128,2048]{1,0:T(8,128)(2,1)}, bf16[128,1024]{1,0:T(8,128)(2,1)}, f32[6,16,128]{2,1,0:T(8,128)}, f32[16,128]{1,0:T(8,128)}) custom-call(bf16[128,2048]{1,0:T(8,128)(2,1)S(1)} %get-tuple-element.11.gq_ref, bf16[128,2048]{1,0:T(8,128)(2,1)S(1)} %get-tuple-element.12.gk_ref, ...), custom_call_target="tpu_custom_call" | custom-call | tf_op jit(solution)/shard_map/pallas_call | solution.py:1412

commit v8 on v7

--- a/solution.py
+++ b/solution.py
@@ -658,24 +658,13 @@
     starts = jnp.broadcast_to(ds_ref[...].astype(F32), (8, tok))
     both = jnp.concatenate([lg_ref[...], starts], axis=0)
     cum_all = dot_exact(both, tri)
-    cum_t = jnp.transpose(
-        jnp.concatenate([cum_all, jnp.zeros((dk - heads - 8, tok), F32)], axis=0)
-    )
     cum = cum_all[:heads]
     reset = cum_all[heads : heads + 1]
-    reset_col = cum_t[:, heads : heads + 1]
-    bias_s[...] = jnp.where((rows_i <= cols_i) & (reset == reset_col), 0.0, -1e30)
-    end = cum[:, tok - 1 : tok]
+    end_sum = cum[:, tok - 1 : tok]
     reset_end = reset[:, tok - 1 : tok]
     cum_s[...] = cum
     lead_s[...] = jnp.where(reset == 0, jnp.exp(cum), 0.0)
-    tail_s[...] = jnp.where(reset == reset_end, jnp.exp(end - cum), 0.0)
-    lane_row = lax.broadcasted_iota(jnp.int32, (1, dk), 1)
-    end_row = jnp.where(lane_row < heads, cum_t[tok - 1 : tok, :], 0.0)
-    decs[0] = jnp.where(reset_end == 0, jnp.exp(end_row), 0.0)
-    for h in range(heads):
-        col_s[h] = jnp.broadcast_to(cum_t[:, h : h + 1], (tok, tok))
-
+    tail_s[...] = jnp.where(reset == reset_end, jnp.exp(end_sum - cum), 0.0)
     def states(p, _):
         lanes = pl.ds(pl.multiple_of(p * dk, dk), dk)
         vt = jnp.transpose(v_ref[:, lanes].astype(F32))
@@ -774,7 +763,7 @@
         there = pl.ds(mine + n * piece, piece)
         return remote(sum_q.at[here], lvl.at[2, there], y_send.at[n], y_recv.at[n], 2)
 
-    late = range(pieces - group // piece, pieces)
+    late = range(pieces - 2, pieces)
 
     def early_copy(n):
         return remote(
@@ -795,14 +784,27 @@
         part = lvl.at[j, of(base, c)]
         return remote(part, part, f_send.at[j - 1, c], f_recv.at[j - 1, c], 0)
 
-    dec_copy(0).start()
     for c in range(2):
         a_copy(c).start()
+    lane_h = lax.broadcasted_iota(jnp.int32, (heads, dk), 1)
+    head_h = lax.broadcasted_iota(jnp.int32, (heads, dk), 0)
+    decay_all = jnp.where(reset_end == 0, jnp.exp(end_sum), 0.0)
+    decs[0] = jnp.sum(jnp.where(lane_h == head_h, decay_all, 0.0), axis=0, keepdims=True)
+    dec_copy(0).start()
     states_from(far_pair + 2)
     for c in range(2, chunks):
         a_copy(c).start()
     states_from(own_pair)
     states_from(own_pair + 2)
+    cum_t = jnp.transpose(
+        jnp.concatenate([cum_all, jnp.zeros((dk - heads - 8, tok), F32)], axis=0)
+    )
+    bias_s[...] = jnp.where(
+        (rows_i <= cols_i) & (reset == cum_t[:, heads : heads + 1]), 0.0, -1e30
+    )
+    for h in range(heads):
+        col_s[h] = jnp.broadcast_to(cum_t[:, h : h + 1], (tok, tok))
+
 
     span_of = lax.broadcasted_iota(jnp.int32, (1, tok), 1) // SPAN
 
@@ -871,41 +873,38 @@
     def local_pairs(first, last):
         lax.fori_loop(first, last, local, 0, unroll=2)
 
+    def x_item(n, act):
+        if n < late[0]:
+            act(xa_copy(n))
+            return
+
+        @pl.when(y == 0)
+        def _():
+            if n < pieces:
+                act(xa_copy(n))
+            elif n < 2 * pieces and (n - pieces not in late or act is end):
+
+                @pl.when(x == 1)
+                def _():
+                    act(xb_copy(n - pieces))
+
+        if n - late[0] < pieces:
+
+            @pl.when(y == 1)
+            def _():
+                act(xb_copy(n - late[0]))
+
+    def begin(copy):
+        copy.start()
+
+    def end(copy):
+        copy.wait_send()
+
     def x_start(n):
-        if n in late:
-
-            @pl.when(y == 0)
-            def _():
-                xa_copy(n).start()
-
-        elif n < pieces:
-            xa_copy(n).start()
-        elif n - pieces in late:
-
-            @pl.when((y == 1) & (first_chip == 0))
-            def _():
-                xb_copy(n - pieces).start()
-
-        elif n < 2 * pieces:
-
-            @pl.when(first_chip == 0)
-            def _():
-                xb_copy(n - pieces).start()
+        x_item(n, begin)
 
     def x_sent(n):
-        if n in late:
-
-            @pl.when(y == 0)
-            def _():
-                xa_copy(n).wait_send()
-
-        elif n < pieces:
-            xa_copy(n).wait_send()
-        else:
-
-            @pl.when(first_chip == 0)
-            def _():
-                xb_copy(n - pieces).wait_send()
+        x_item(n, end)
 
     ahead = 5
 
@@ -922,7 +921,7 @@
         a_copy(c).wait_recv()
         combine(0, c, lambda r: st[kind_a, mine + r], lambda r: got_a[r], sum_a)
         for n in pieces_of(c):
-            if n < 3:
+            if n < 2:
                 x_start(n)
         if c == 1:
             dec_copy(1).start()
@@ -932,13 +931,20 @@
                 for n in range(chunks):
                     b_copy(n).start()
 
-    @pl.when(y == 1)
-    def _():
-        for n in late:
+    for n in range(2, ahead):
+        if n - 2 < len(late):
+
+            @pl.when(y == 1)
+            def _():
+                early_copy(late[n - 2]).start()
+
+        x_start(n)
+    for n in late[ahead - 2 :]:
+
+        @pl.when(y == 1)
+        def _():
             early_copy(n).start()
 
-    for n in range(3, ahead):
-        x_start(n)
     local_pairs(0, 4)
 
     @pl.when(first_chip == 0)
@@ -994,6 +1000,15 @@
             def _():
                 f_copy(1, mine, n * piece // group).start()
 
+    def pass_on(ns):
+        @pl.when(first_chip == 1)
+        def _():
+            for n in ns:
+                early_copy(n).wait_recv()
+                relay_copy(n).start()
+                for r in range(n * piece, (n + 1) * piece):
+                    lvl[2, mine + r] = jnp.zeros((dv, dk), F32)
+
     turn(0)
     local_pairs(6, pairs)
     x_next(4)
@@ -1004,18 +1019,12 @@
     turn(3)
     x_next(7)
     turn(4)
-
-    @pl.when(first_chip == 1)
-    def _():
-        for n in late:
-            early_copy(n).wait_recv()
-            relay_copy(n).start()
-            for r in range(n * piece, (n + 1) * piece):
-                lvl[2, mine + r] = jnp.zeros((dv, dk), F32)
+    pass_on(late[:1])
 
     x_next(8)
     turn(5)
     turn(6)
+    pass_on(late[1:])
     x_next(9)
     x_next(10)
     turn(7)
@@ -1084,10 +1093,10 @@
     mix_s[3, 0] = d_cross
     mix_s[3, 1] = d_self * d_pair
 
-    def join_late():
+    def join_late(ns):
         @pl.when(second_chip == 1)
         def _():
-            for n in late:
+            for n in ns:
                 early_copy(n).wait_recv()
                 relay_copy(n).wait_recv()
                 for r in range(n * piece, (n + 1) * piece):
@@ -1101,22 +1110,26 @@
 
     for n in range(2):
         p_copy(n).wait_recv()
+    def finish_far(c):
+        for j in (1, 2):
+            f_copy(j, theirs, c).wait_recv()
+        finish_drift(far_pair + c)
+
     for c in range(chunks):
         for n in ((), (), (), ())[c]:
             x_next(n)
-        if c == chunks - 1:
-
-            @pl.when(y == 1)
-            def _(c=c):
-                for n in pieces_of(c):
+        if c == 0:
+            join_late(late)
+        for n in pieces_of(c):
+            if n in late:
+
+                @pl.when(y == 1)
+                def _():
                     y_copy(n).wait_recv()
 
-        else:
-            for n in pieces_of(c):
+            else:
                 y_copy(n).wait_recv()
         f_copy(2, mine, c).start()
-        if c == 1:
-            join_late()
 
         @pl.when(second_chip == 0)
         def _(c=c):
@@ -1133,9 +1146,9 @@
                     device_id_type=MESH,
                 )
         finish_drift(own_pair + c)
-        for j in (1, 2):
-            f_copy(j, theirs, c).wait_recv()
-        finish_drift(far_pair + c)
+        if c > 0:
+            finish_far(c - 1)
+    finish_far(chunks - 1)
 
     later = (rows_i >= cols_i).astype(BF16)
     local_tail = dot_exact(drift_s[...], later)
@@ -1359,7 +1372,7 @@
             vmem((half,) + block, F32),
             vmem((half,) + block, F32),
             vmem((bits + 1, heads) + block, F32),
-            vmem((2, group) + block, F32),
+            vmem((2, 2) + block, F32),
             vmem((6, 1, dk), F32),
             dma((7,)),
             dma((chunks,)),
@@ -1376,8 +1389,8 @@
             dma((half,)),
             dma((2, chunks)),
             dma((2, chunks)),
-            dma((group,)),
-            dma((group,)),
+            dma((2,)),
+            dma((2,)),
             dma((3,)),
             dma((3,)),
             dma((1,)),

time: 29.4 us -> 27.8 us (0.946)
  Pallas kernels: 28.5 us -> 26.9 us
    pallas_call x1, Pallas kernels: 27.4 us -> 25.8 us  [shards(): pl.pallas_call(functools.partial(body, seq_count, head_count), out_shape=...]
where the time goes in v8:
time: 27.8 us; the launch traced here: 27.6 us
  Pallas kernels  26.9 us (97%)
  between operations  0.64 us (2%)
    pallas_call x1, Pallas kernels, shards(): pl.pallas_call(functools.partial(body, seq_count, head_count), out_shape=...  25.8 us
    pallas_call x1, Pallas kernels, shards(): pl.pallas_call(functools.partial(*writer), out_shape=tuple((jax.ShapeDtyp...  1.11 us

profile of v8, /device:TPU:0, one launch (start us, length us, event | category | flops | bytes accessed | tf_op | source)
XLA Modules:
  0.0 27.6 jit_solution(8696497821987268800)
XLA Ops:
  0.6 25.8 %shard_map.110 = (bf16[128,2048]{1,0:T(8,128)(2,1)S(1)}, bf16[128,2048]{1,0:T(8,128)(2,1)S(1)}, bf16[128,1024]{1,0:T(8,128)(2,1)S(1)}, f32[6,16,128]{2,1,0:T(8,1...) custom-call(bf16[128,2048]{1,0:T(8,128)(2,1)} %q_hbm.1, bf16[128,2048]{1,0:T(8,128)(2,1)} %k_hbm.1, ...), custom_call_target="tpu_custom_call" | custom-call | tf_op jit(solution)/shard_map/pallas_call | solution.py:1416
  26.5 1.1 %shard_map.111 = (bf16[128,2048]{1,0:T(8,128)(2,1)}, bf16[128,2048]{1,0:T(8,128)(2,1)}, bf16[128,1024]{1,0:T(8,128)(2,1)}, f32[6,16,128]{2,1,0:T(8,128)}, f32[16,128]{1,0:T(8,128)}) custom-call(bf16[128,2048]{1,0:T(8,128)(2,1)S(1)} %get-tuple-element.11.gq_ref, bf16[128,2048]{1,0:T(8,128)(2,1)S(1)} %get-tuple-element.12.gk_ref, ...), custom_call_target="tpu_custom_call" | custom-call | tf_op jit(solution)/shard_map/pallas_call | solution.py:1425

commit v9 on v8

--- a/solution.py
+++ b/solution.py
@@ -669,21 +669,29 @@
         lanes = pl.ds(pl.multiple_of(p * dk, dk), dk)
         vt = jnp.transpose(v_ref[:, lanes].astype(F32))
         gt = jnp.transpose(g_ref[:, lanes].astype(F32))
-        vt_s[p] = vt.astype(BF16)
-        gt_s[p] = gt.astype(BF16)
+        made = []
         for i in range(group):
             h = p * group + i
             wide = pl.ds(pl.multiple_of(h * dk, dk), dk)
             part = slice(i * dv, (i + 1) * dv)
             tail = tail_s[pl.ds(h, 1), :]
             lead = lead_s[pl.ds(h, 1), :]
-            st[0, h] = dot_fine(vt[part] * tail, k_ref[:, wide], NN)
             gw = jnp.concatenate(
                 [gt[part] * (lead * lw_ref[l, pl.ds(h, 1), :]) for l in slots], axis=0
             )
-            back = dot_fine(gw, q_ref[:, wide], NN)
+            made.append(
+                (
+                    h,
+                    dot_fine(vt[part] * tail, k_ref[:, wide], NN),
+                    dot_fine(gw, q_ref[:, wide], NN),
+                )
+            )
+        for h, front, back in made:
+            st[0, h] = front
             for n in range(len(slots)):
                 st[1 + n, h] = back[n * dv : (n + 1) * dv]
+        vt_s[p] = vt.astype(BF16)
+        gt_s[p] = gt.astype(BF16)
         return 0
 
     for n in range(2, 7):
@@ -959,7 +967,11 @@
             greet(round_sem.at[r])
     x_next(0)
     x_next(1)
-    p_copy(0).start()
+
+    @pl.when(core == 1)
+    def _():
+        p_copy(0).start()
+
     local_pairs(4, 6)
     dec_copy(1).wait_recv()
     (d_side,) = spread([decs[3]])
@@ -976,7 +988,11 @@
             inner_b = inner_b * ((1.0 - up) * got + up)
     x_next(2)
     x_next(3)
-    p_copy(1).start()
+
+    @pl.when(core == 1)
+    def _():
+        p_copy(1).start()
+
     def turn(n):
         if n in late:
 
@@ -1014,10 +1030,20 @@
     x_next(4)
     turn(1)
     x_next(5)
+
+    @pl.when(core == 0)
+    def _():
+        p_copy(0).start()
+
     turn(2)
     x_next(6)
     turn(3)
     x_next(7)
+
+    @pl.when(core == 0)
+    def _():
+        p_copy(1).start()
+
     turn(4)
     pass_on(late[:1])
 
@@ -1047,26 +1073,36 @@
     def finish_drift(p):
         vt = vt_s[p].astype(F32)
         gt = gt_s[p].astype(F32)
-        for i in range(group):
-            h = p * group + i
+        vg_old = vg_s[p]
+        heads_of = [p * group + i for i in range(group)]
+        held = [incoming(h) for h in heads_of]
+        seen_all, out_all = [], []
+        for h, ((e_high, e_low), (a_high, a_low)) in zip(heads_of, held):
             wide = pl.ds(pl.multiple_of(h * dk, dk), dk)
-            part = slice(i * dv, (i + 1) * dv)
             q = q_ref[:, wide]
             k = k_ref[:, wide]
-            tail = tail_s[pl.ds(h, 1), :]
+            seen_all.append(dot(e_high, q, NT) + dot(e_low, q, NT))
+            out_all.append(dot(a_high, k, NT) + dot(a_low, k, NT))
+        stores = []
+        for i, h in enumerate(heads_of):
+            part = slice(i * dv, (i + 1) * dv)
             lead = lead_s[pl.ds(h, 1), :]
-            (e_high, e_low), (a_high, a_low) = incoming(h)
-            seen = dot(e_high, q, NT) + dot(e_low, q, NT)
             drift = drift_s[pl.ds(h, 1), :]
+            rows = []
             for n, l in enumerate(slots):
                 level = lead * jnp.sum(
-                    seen[n * dv : (n + 1) * dv] * gt[part], axis=0, keepdims=True
+                    seen_all[i][n * dv : (n + 1) * dv] * gt[part], axis=0, keepdims=True
                 )
+                rows.append(level)
+                drift = drift + lw_ref[l, pl.ds(h, 1), :] * level
+            vg = vg_old[part] + tail_s[pl.ds(h, 1), :] * out_all[i]
+            drift = drift - jnp.sum(vg * vt[part], axis=0, keepdims=True)
+            stores.append((drift, vg, rows))
+        for h, (drift, vg, rows) in zip(heads_of, stores):
+            drift_s[pl.ds(h, 1), :] = drift
+            for l, level in zip(slots, rows):
                 gl_ref[l, pl.ds(h, 1), :] = level
-                drift = drift + lw_ref[l, pl.ds(h, 1), :] * level
-            vg = vg_s[p, part] + tail * (dot(a_high, k, NT) + dot(a_low, k, NT))
-            drift_s[pl.ds(h, 1), :] = drift - jnp.sum(vg * vt[part], axis=0, keepdims=True)
-            vg_s[p, part] = vg
+        vg_s[p] = jnp.concatenate([vg for _, vg, _ in stores], axis=0)
 
     def finish_out(p):
         lanes = pl.ds(pl.multiple_of(p * dk, dk), dk)

time: 27.8 us -> 27.8 us (level)
  no operation moved by 1% of the time
where the time goes in v9:
time: 27.8 us; the launch traced here: 27.6 us
  Pallas kernels  26.9 us (97%)
  between operations  0.64 us (2%)
    pallas_call x1, Pallas kernels, shards(): pl.pallas_call(functools.partial(body, seq_count, head_count), out_shape=...  25.8 us
    pallas_call x1, Pallas kernels, shards(): pl.pallas_call(functools.partial(*writer), out_shape=tuple((jax.ShapeDtyp...  1.11 us

profile of v9, /device:TPU:0, one launch (start us, length us, event | category | flops | bytes accessed | tf_op | source)
XLA Modules:
  0.0 27.6 jit_solution(13111838910636980636)
XLA Ops:
  0.6 25.8 %shard_map.110 = (bf16[128,2048]{1,0:T(8,128)(2,1)S(1)}, bf16[128,2048]{1,0:T(8,128)(2,1)S(1)}, bf16[128,1024]{1,0:T(8,128)(2,1)S(1)}, f32[6,16,128]{2,1,0:T(8,1...) custom-call(bf16[128,2048]{1,0:T(8,128)(2,1)} %q_hbm.1, bf16[128,2048]{1,0:T(8,128)(2,1)} %k_hbm.1, ...), custom_call_target="tpu_custom_call" | custom-call | tf_op jit(solution)/shard_map/pallas_call | solution.py:1452
  26.5 1.1 %shard_map.111 = (bf16[128,2048]{1,0:T(8,128)(2,1)}, bf16[128,2048]{1,0:T(8,128)(2,1)}, bf16[128,1024]{1,0:T(8,128)(2,1)}, f32[6,16,128]{2,1,0:T(8,128)}, f32[16,128]{1,0:T(8,128)}) custom-call(bf16[128,2048]{1,0:T(8,128)(2,1)S(1)} %get-tuple-element.11.gq_ref, bf16[128,2048]{1,0:T(8,128)(2,1)S(1)} %get-tuple-element.12.gk_ref, ...), custom_call_target="tpu_custom_call" | custom-call | tf_op jit(solution)/shard_map/pallas_call | solution.py:1461
